TPU v7x, 32 devices: a whole 2x2x4 slice. The times are simulated.
32 devices in a mesh: parts: 2 (over x), pts: 16 (over z, y, core).
Axes of the slice: x: 2, y: 2, z: 4, core: 2. Of those that a mesh axis runs over, the one named last changes fastest.
Arguments:
- grid_weights: float32 [256, 128, 128], P(('parts', 'pts')), parts along dimension 0, may hold values from -6 to 6
- direction: float32 [256, 128, 128], P(('parts', 'pts')), parts along dimension 0, may hold values from -6 to 6
- kern_x: float32 [128, 128], replicated
- kern_y: float32 [128, 128], replicated
- kern_z: float32 [128, 128], replicated
- interp: bfloat16 [4096, 128, 256], P(('parts', 'pts')), parts along dimension 0, may hold values from -4 to 4
- block_corner: int32 [3, 4096], P(None, ('parts', 'pts')), parts along dimension 1, may hold values from 0 to 120, as said below
- block_offsets: int32 [4096, 256], P(('parts', 'pts')), parts along dimension 0, may hold values from 0 to 2047, as said below
- labels: int32 [4096, 128], P(('parts', 'pts')), parts along dimension 0, may hold values 0 or 1
- trial_steps: float32 [5], replicated, may hold values from 0.05 to 2
- accept: int32 [1], replicated, may hold values from 0 to 4
Outputs:
- new_weights: float32 [256, 128, 128], P(('parts', 'pts')), parts along dimension 0
- grid_gradient: float32 [256, 128, 128], P(('parts', 'pts')), parts along dimension 0
- curvature: float32 [4096, 128], P(('parts', 'pts')), parts along dimension 0
- trial_objective: float32 [10], P('parts'), parts along dimension 0
- trial_slope: float32 [10], P('parts'), parts along dimension 0
There are 2 independent parts, one for each index of `parts`. A program takes and returns all parts, laid end to end along the dimension named above; an argument that names none is the same for every part. Nothing has to cross between parts.
Inputs may be any that keep to these rules, and one draw needn't show every extreme that they name: `block_corner`: row 0 lies in 0 to 112, row 1 in 0 to 112, row 2 in 0 to 120. `block_offsets`: the 256 offsets of one block are distinct.
All inputs are finite; a program needn't handle non-finite values. No bound on the sum of `labels` on one device may be relied on, other than what follows from the above.
Results may differ from a plain program's by a relative error of at most 0.0075.
The roundings to bfloat16 on the way count: a program that leaves them out, or rounds other values in their place, can miss the bound.
Values may be sent and summed in bfloat16 or wider, within the bound.
A program may use at most 128 MiB of HBM per device.

v0:
```python
import functools

import jax
import jax.numpy as jnp
from jax import lax
from jax.experimental import pallas as pl
from jax.experimental.pallas import tpu as pltpu
from jax.sharding import PartitionSpec as P

BOXX = 16
BOXY = 16
BOXZ = 8
NTRIAL = 5
PACK = 16
VMEM_BYTES = 62 * 1024 * 1024
UP, DOWN, SIDE, TWIN = range(4)

HIGHEST = lax.Precision.HIGHEST
F32 = jnp.float32
BF16 = jnp.bfloat16
NT = (((1,), (1,)), ((), ()))
MESH = pl.DeviceIdType.MESH


def high_part(value):
    return lax.reduce_precision(value, 8, 7)


def plane_mix(fields_zc, kern_y, kern_z):
    inner = jnp.einsum("zc,fabc->zfab", kern_z, fields_zc, precision=HIGHEST)
    return jnp.einsum("zfab,yb->zfay", inner, kern_y, precision=HIGHEST).astype(BF16)


def widen_kern(kern_x, devices, slab, group):
    size_x = kern_x.shape[0]
    parts = kern_x.reshape(1, size_x, devices, 1, slab)
    same = jnp.eye(group, dtype=F32).reshape(group, 1, 1, group, 1)
    wide = (parts * same).reshape(group * size_x, devices * group * slab)
    high = high_part(wide)
    return high.astype(BF16), (wide - high).astype(BF16)


class Place:
    def __init__(self, devices):
        me = lax.axis_index("pts")
        self.devices = devices
        self.depths = devices // 4
        self.me = me
        self.core = lax.rem(me, 2)
        self.side = lax.rem(lax.div(me, 2), 2)
        self.depth = lax.div(me, 4)

    def slot(self, depth, side, core):
        return (depth * 2 + side) * 2 + core

    def target(self, kind):
        if kind == UP:
            return self.slot(self.depth + 1, self.side, self.core)
        if kind == DOWN:
            return self.slot(self.depth - 1, self.side, self.core)
        if kind == SIDE:
            return self.slot(self.depth, 1 - self.side, self.core)
        return self.slot(self.depth, self.side, 1 - self.core)

    def greet(self):
        barrier = pltpu.get_barrier_semaphore()

        def tell(kind):
            pl.semaphore_signal(
                barrier, inc=1, device_id={"pts": self.target(kind)}, device_id_type=MESH
            )

        tell(SIDE)
        tell(TWIN)

        @pl.when(self.depth + 1 < self.depths)
        def _():
            tell(UP)

        @pl.when(self.depth > 0)
        def _():
            tell(DOWN)

        above = jnp.where(self.depth + 1 < self.depths, 1, 0)
        below = jnp.where(self.depth > 0, 1, 0)
        pl.semaphore_wait(barrier, 2 + above + below)


class Relay:
    def __init__(self, place, own, buf, send, recv):
        self.place = place
        self.own = own
        self.buf = buf
        self.send = send
        self.recv = recv
        self.pieces = recv.shape[1]
        self.size = own.shape[0] // self.pieces

    def copy(self, slot, piece, kind, mine=False):
        rows = pl.ds(piece * self.size, self.size)
        landing = self.buf.at[slot, rows]
        return pltpu.make_async_remote_copy(
            src_ref=self.own.at[rows] if mine else landing,
            dst_ref=landing,
            send_sem=self.send.at[kind, lax.div(slot, 2), piece],
            recv_sem=self.recv.at[slot, piece],
            device_id={"pts": self.place.target(kind)},
            device_id_type=MESH,
        )

    def take(self, slot, piece):
        self.copy(slot, piece, TWIN).wait_recv()

    def line_sends(self, depth, piece, act, mine=False):
        here = self.place
        slot = here.slot(depth, here.side, here.core)

        @pl.when((depth <= here.depth) & (here.depth + 1 < here.depths))
        def _():
            act(self.copy(slot, piece, UP, mine))

        @pl.when((depth >= here.depth) & (here.depth > 0))
        def _():
            act(self.copy(slot, piece, DOWN, mine))

        act(self.copy(slot, piece, SIDE, mine))
        act(self.copy(slot, piece, TWIN, mine))

    def side_sends(self, depth, piece, act):
        here = self.place
        act(self.copy(here.slot(depth, 1 - here.side, here.core), piece, TWIN))

    def start_own(self, piece):
        self.line_sends(self.place.depth, piece, lambda c: c.start(), mine=True)

    def line_events(self, piece, far):
        here = self.place
        for way in (-1, 1):
            depth = here.depth + way * far

            @pl.when((far > 0) & (depth >= 0) & (depth < here.depths))
            def _():
                self.take(here.slot(depth, here.side, here.core), piece)
                self.line_sends(depth, piece, lambda c: c.start())

    def side_events(self, piece, far):
        here = self.place
        for way in (-1, 1):
            depth = here.depth + way * far
            wanted = (depth >= 0) & (depth < here.depths)
            if way > 0:
                wanted = wanted & (far > 0)

            @pl.when(wanted)
            def _():
                self.take(here.slot(depth, 1 - here.side, here.core), piece)
                self.side_sends(depth, piece, lambda c: c.start())

    def twin_events(self, piece):
        here = self.place

        def one(pair, carry):
            self.take(pair * 2 + (1 - here.core), piece)
            return carry

        lax.fori_loop(0, here.devices // 2, one, 0)

    def run(self, work=None, mix=None, tail=None):
        depths = self.place.depths

        def one(piece, carry):
            @pl.when(piece + 1 < self.pieces)
            def _():
                self.start_own(piece + 1)

            def near(far, carry):
                self.line_events(piece, far)

                @pl.when(piece > 0)
                def _():
                    self.side_events(piece - 1, far)

                if work is not None:
                    work(piece * depths + far)
                return carry

            lax.fori_loop(0, depths, near, 0)

            @pl.when(piece > 0)
            def _():
                self.twin_events(piece - 1)
                if mix is not None:
                    mix(piece - 1)

            return carry

        lax.fori_loop(0, self.pieces, one, 0)
        if tail is not None:
            tail()

        def last(far, carry):
            self.side_events(self.pieces - 1, far)
            return carry

        lax.fori_loop(0, depths, last, 0)
        self.twin_events(self.pieces - 1)
        if mix is not None:
            mix(self.pieces - 1)

    def finish(self):
        def one(step, carry):
            piece = lax.div(step, self.place.depths)
            depth = lax.rem(step, self.place.depths)
            self.line_sends(depth, piece, lambda c: c.wait_send())
            self.side_sends(depth, piece, lambda c: c.wait_send())
            return carry

        lax.fori_loop(0, self.pieces * self.place.depths, one, 0)


def relay_sems(devices, pieces):
    return [
        pltpu.SemaphoreType.DMA((4, devices // 2, pieces)),
        pltpu.SemaphoreType.DMA((devices, pieces)),
    ]


def mix_depth(planes_ref, kh_ref, kl_ref, image, group, size_x, first, count):
    devices, _, pack, lanes = planes_ref.shape

    def one(step, carry):
        at = first + step * 2
        pair = [planes_ref[:, at + t].reshape(devices * pack, lanes) for t in range(2)]
        rhs = jnp.concatenate(pair, axis=1)
        mixed = jnp.dot(kh_ref[...], rhs, preferred_element_type=F32)
        mixed = mixed + jnp.dot(kl_ref[...], rhs, preferred_element_type=F32)
        for t in range(2):
            for g in range(group):
                image[(at + t) * group + g] = mixed[
                    g * size_x : (g + 1) * size_x, t * lanes : (t + 1) * lanes
                ]
        return carry

    lax.fori_loop(0, count // 2, one, 0)


def pick_values(image, corner_ref, y_ref, row_ref, block):
    size_y = image.shape[-1]
    cols = y_ref.shape[-1]
    box_rows = BOXZ * BOXX
    at_z = corner_ref[2, block]
    at_x = corner_ref[0, block]
    box = image[pl.ds(at_z, BOXZ), pl.ds(at_x, BOXX), :]
    box = box.reshape(box_rows, size_y).astype(BF16)
    y_line = lax.broadcasted_iota(jnp.int32, (size_y, cols), 0)
    pick_y = jnp.where(y_line == y_ref[pl.ds(block, 1), :], 1.0, 0.0).astype(BF16)
    lines = jnp.dot(box, pick_y, preferred_element_type=F32)
    row_line = lax.broadcasted_iota(jnp.int32, (box_rows, cols), 0)
    line = jnp.where(row_line == row_ref[pl.ds(block, 1), :], lines, 0.0)
    value = jnp.sum(line, axis=0, keepdims=True)
    return jnp.broadcast_to(value, (8, cols)).astype(BF16)


def interpolate_blocks(image, corner_ref, y_ref, row_ref, interp, out_ref, first, count):
    unroll = min(8, count)

    def some(part, carry):
        for k in range(unroll):
            block = first + part * unroll + k
            values = pick_values(image, corner_ref, y_ref, row_ref, block)
            line = lax.dot_general(values, interp[block], NT, preferred_element_type=F32)
            out_ref[pl.ds(block, 1), :] = line[0:1]
        return carry

    lax.fori_loop(0, count // unroll, some, 0)


def log_sigmoid(value):
    return jnp.minimum(value, 0.0) - jnp.log1p(jnp.exp(-jnp.abs(value)))


def forward_kernel(
    group,
    corner_ref,
    chosen_ref,
    trial_ref,
    own_u,
    own_d,
    offs_ref,
    kh_ref,
    kl_ref,
    y_ref,
    row_ref,
    labels_ref,
    weights_ref,
    direction_ref,
    interp_ref,
    prob_ref,
    sums_ref,
    all_offs,
    all_terms,
    buf_u,
    buf_d,
    image_u,
    image_d,
    interp,
    latent_ref,
    slope_ref,
    res_ref,
    term_ref,
    own_terms,
    local_sem,
    *sems,
):
    devices, units, pack, lanes = buf_u.shape
    blocks, per_block = labels_ref.shape
    slab = pack // group
    size_x = image_u.shape[1]
    place = Place(devices)
    load = pltpu.make_async_copy(interp_ref, interp, local_sem)
    load.start()
    u = Relay(place, own_u, buf_u, sems[0], sems[1])
    d = Relay(place, own_d, buf_d, sems[2], sems[3])
    o = Relay(place, offs_ref, all_offs, sems[4], sems[5])
    t = Relay(place, own_terms, all_terms, sems[6], sems[7])
    place.greet()
    u.start_own(0)
    buf_u[place.me] = own_u[...]
    buf_d[place.me] = own_d[...]
    all_offs[place.me] = offs_ref[...]

    def mixer(buf, image):
        return lambda piece: mix_depth(
            buf, kh_ref, kl_ref, image, group, size_x, piece * u.size, u.size
        )

    u.run(mix=mixer(buf_u, image_u), tail=lambda: d.start_own(0))
    load.wait()
    steps = u.pieces * place.depths
    some = blocks // steps

    def early(step):
        interpolate_blocks(
            image_u, corner_ref, y_ref, row_ref, interp, latent_ref, step * some, some
        )

    d.run(work=early, mix=mixer(buf_d, image_d), tail=lambda: o.start_own(0))
    part = blocks // place.depths

    def late(step):
        interpolate_blocks(
            image_d, corner_ref, y_ref, row_ref, interp, slope_ref, step * part, part
        )

    o.run(work=late)
    slope = slope_ref[...]
    latent = latent_ref[...]
    prob = jax.nn.sigmoid(latent + chosen_ref[0] * slope)
    prob_ref[...] = prob
    target = labels_ref[...].astype(F32)
    res_ref[...] = (target - prob).astype(BF16).astype(F32)
    unroll = 8

    def back(step, carry):
        for k in range(unroll):
            block = step * unroll + k
            row = jnp.broadcast_to(res_ref[pl.ds(block, 1), :], (8, per_block))
            term = jnp.dot(row.astype(BF16), interp[block], preferred_element_type=F32)
            term_ref[pl.ds(block, 1), :] = term[0:1]
        return carry

    lax.fori_loop(0, blocks // unroll, back, 0)
    own_terms[...] = term_ref[...].astype(BF16)
    all_terms[place.me] = own_terms[...]
    u.finish()
    d.finish()
    o.finish()
    at = pl.multiple_of(place.me * slab, slab)
    image_w = image_u[:, pl.ds(at, slab), :]
    image_t = image_d[:, pl.ds(at, slab), :]
    sums = [
        jnp.sum(weights_ref[...] * image_w),
        jnp.sum(direction_ref[...] * image_w),
        jnp.sum(direction_ref[...] * image_t),
    ]
    t.start_own(0)
    signed = 2.0 * target - 1.0
    loglik, descent = [], []
    for k in range(NTRIAL):
        at_trial = latent + trial_ref[k] * slope
        loglik.append(jnp.sum(log_sigmoid(signed * at_trial)))
        descent.append(jnp.sum((target - jax.nn.sigmoid(at_trial)) * slope))
    lane = lax.broadcasted_iota(jnp.int32, sums_ref.shape, 1)
    row = jnp.zeros(sums_ref.shape, F32)
    for k, value in enumerate(loglik + descent + sums):
        row = jnp.where(lane == k, value, row)
    sums_ref[...] = row
    t.run()
    t.finish()


def bend_kernel(
    group,
    corner_ref,
    own_ref,
    split_ref,
    kh_ref,
    kl_ref,
    y_ref,
    row_ref,
    prob_ref,
    interp_ref,
    out_ref,
    total_ref,
    buf,
    all_split,
    image,
    interp,
    local_sem,
    *sems,
):
    devices = buf.shape[0]
    blocks = prob_ref.shape[0]
    size_x = image.shape[1]
    place = Place(devices)
    load = pltpu.make_async_copy(interp_ref, interp, local_sem)
    load.start()
    b = Relay(place, own_ref, buf, sems[0], sems[1])
    s = Relay(place, split_ref, all_split, sems[2], sems[3])
    place.greet()
    b.start_own(0)
    buf[place.me] = own_ref[...]
    all_split[place.me] = split_ref[...]
    b.run(
        mix=lambda piece: mix_depth(
            buf, kh_ref, kl_ref, image, group, size_x, piece * b.size, b.size
        ),
        tail=lambda: s.start_own(0),
    )
    load.wait()
    part = blocks // place.depths

    def late(step):
        interpolate_blocks(
            image, corner_ref, y_ref, row_ref, interp, out_ref, step * part, part
        )

    s.run(work=late)
    total_ref[...] = jnp.sum(all_split[...].astype(F32), axis=0)
    prob = prob_ref[...]
    out_ref[...] = prob * (1.0 - prob) * out_ref[...]
    b.finish()
    s.finish()


def scatter_kernel(slab, unroll, ids_ref, count_ref, z_ref, y_ref, key_ref, term_ref, out_ref):
    cols = y_ref.shape[-1]
    size_y = out_ref.shape[-1]
    rows = BOXZ * slab
    out_ref[...] = jnp.zeros_like(out_ref)

    def some(part, carry):
        sums = []
        for k in range(unroll):
            block = ids_ref[part * unroll + k]
            row_line = lax.broadcasted_iota(jnp.int32, (rows, cols), 0)
            y_line = lax.broadcasted_iota(jnp.int32, (size_y, cols), 0)
            wanted = row_line == key_ref[pl.ds(block, 1), :]
            left = jnp.where(wanted, term_ref[pl.ds(block, 1), :], 0.0).astype(BF16)
            right = jnp.where(y_line == y_ref[pl.ds(block, 1), :], 1.0, 0.0).astype(BF16)
            sums.append((block, lax.dot_general(left, right, NT, preferred_element_type=F32)))
        for block, piece in sums:
            at = pl.multiple_of(z_ref[block] * slab, slab)
            out_ref[pl.ds(at, rows), :] += piece
        return carry

    lax.fori_loop(0, lax.div(count_ref[0] + unroll - 1, unroll), some, 0)


def whole(shape):
    return pl.BlockSpec(
        shape, lambda i, *_: (0,) * len(shape), pipeline_mode=pl.Buffered(buffer_count=1)
    )


def body(
    grid_weights,
    direction,
    kern_x,
    kern_y,
    kern_z,
    interp,
    block_corner,
    block_offsets,
    labels,
    trial_steps,
    accept,
):
    slab, size_y, size_z = grid_weights.shape
    size_x = kern_x.shape[0]
    devices = lax.axis_size("pts")
    me = lax.axis_index("pts")
    blocks, cols = block_offsets.shape
    per_block = interp.shape[1]
    points = blocks * per_block * devices
    group = max(1, PACK // slab)
    pack = group * slab
    unroll = 8
    units = size_z // group
    pieces = max(1, 64 // devices)

    spare = jnp.pad(block_corner, ((0, PACK - 3), (0, cols - blocks)))
    sent = jnp.concatenate([block_offsets, spare], axis=0).astype(jnp.int16)
    planes_w, planes_d = (
        plane_mix(field[None], kern_y, kern_z).reshape(units, pack, size_y)
        for field in (grid_weights, direction)
    )
    kern_high, kern_low = widen_kern(kern_x, devices, slab, group)
    y_cell = block_corner[1][:, None] + block_offsets // BOXZ % BOXY
    box_row = block_offsets % BOXZ * BOXX + block_offsets // (BOXY * BOXZ)
    chosen = jnp.sum(jnp.where(jnp.arange(NTRIAL) == accept[0], trial_steps, 0.0))
    weights_t = jnp.transpose(grid_weights, (2, 0, 1))
    direction_t = jnp.transpose(direction, (2, 0, 1))

    smem = pl.BlockSpec(memory_space=pltpu.SMEM)
    vmem = pl.BlockSpec(memory_space=pltpu.VMEM)
    hbm = pl.BlockSpec(memory_space=pl.ANY)
    planes_scratch = pltpu.VMEM((devices, units, pack, size_y), BF16)
    image_scratch = pltpu.VMEM((size_z, size_x, size_y), F32)
    interp_scratch = pltpu.VMEM(interp.shape, BF16)
    point_scratch = pltpu.VMEM((blocks, per_block), F32)
    point_shape = jax.ShapeDtypeStruct((blocks, per_block), F32)

    probability, sums, everyone, terms = pl.pallas_call(
        functools.partial(forward_kernel, group),
        in_specs=[smem] * 3 + [vmem] * 10 + [hbm],
        out_specs=[vmem] * 4,
        out_shape=[
            point_shape,
            jax.ShapeDtypeStruct((8, 128), F32),
            jax.ShapeDtypeStruct((devices,) + sent.shape, jnp.int16),
            jax.ShapeDtypeStruct((devices, blocks, cols), BF16),
        ],
        scratch_shapes=[
            planes_scratch,
            planes_scratch,
            image_scratch,
            image_scratch,
            interp_scratch,
            point_scratch,
            point_scratch,
            point_scratch,
            pltpu.VMEM((blocks, cols), F32),
            pltpu.VMEM((blocks, cols), BF16),
            pltpu.SemaphoreType.DMA,
            *relay_sems(devices, pieces),
            *relay_sems(devices, pieces),
            *relay_sems(devices, 1),
            *relay_sems(devices, 1),
        ],
        compiler_params=pltpu.CompilerParams(
            vmem_limit_bytes=VMEM_BYTES, collective_id=0, has_side_effects=True
        ),
        name="forward",
    )(
        block_corner,
        chosen.reshape(1),
        trial_steps,
        planes_w,
        planes_d,
        sent,
        kern_high,
        kern_low,
        y_cell,
        box_row,
        labels,
        weights_t,
        direction_t,
        interp,
    )
    terms = terms.reshape(devices * blocks, cols).astype(F32)

    far_offsets = everyone[:, :blocks].astype(jnp.int32).reshape(devices * blocks, cols)
    far = everyone[:, blocks : blocks + 3, :blocks].astype(jnp.int32)
    far_x, far_y, far_z = (far[:, k].reshape(-1) for k in range(3))
    x_from = far_x - me * slab
    far_cell = x_from[:, None] + far_offsets // (BOXY * BOXZ)
    inside = (far_cell >= 0) & (far_cell < slab)
    key = jnp.where(inside, far_offsets % BOXZ * slab + far_cell, -1)
    far_line = far_y[:, None] + far_offsets // BOXZ % BOXY
    total = devices * blocks
    touches = (x_from < slab) & (x_from > -BOXX)
    ranks = jnp.arange(total, dtype=jnp.int32)
    ids = lax.sort(jnp.where(touches, ranks, ranks + total))
    ids = jnp.where(ids >= total, ids - total, ids)
    touched = jnp.sum(touches.astype(jnp.int32)).reshape(1)

    spread = pl.pallas_call(
        functools.partial(scatter_kernel, slab, unroll),
        grid_spec=pltpu.PrefetchScalarGridSpec(
            num_scalar_prefetch=3,
            grid=(1,),
            in_specs=[whole((total, cols))] * 3,
            out_specs=pl.BlockSpec((size_z * slab, size_y), lambda i, *_: (0, 0)),
        ),
        out_shape=jax.ShapeDtypeStruct((size_z * slab, size_y), F32),
        compiler_params=pltpu.CompilerParams(vmem_limit_bytes=VMEM_BYTES),
        name="spread",
    )(ids, touched, far_z, far_line, key, terms)

    new_weights = grid_weights + chosen * direction
    grid_gradient = (
        jnp.transpose(spread.reshape(size_z, slab, size_y), (1, 2, 0)) - new_weights
    )

    sums = sums[0]
    first = high_part(sums)
    second = high_part(sums - first)
    third = sums - first - second
    split = jnp.stack([first, second, third]).astype(BF16)
    split = jnp.pad(split, ((0, PACK - 3), (0, 0)))

    bend_planes = plane_mix(grid_gradient[None], kern_y, kern_z)
    bend_planes = bend_planes.reshape(units, pack, size_y)
    curvature, totals = pl.pallas_call(
        functools.partial(bend_kernel, group),
        in_specs=[smem] + [vmem] * 7 + [hbm],
        out_specs=[vmem] * 2,
        out_shape=[point_shape, jax.ShapeDtypeStruct((PACK, 128), F32)],
        scratch_shapes=[
            planes_scratch,
            pltpu.VMEM((devices, PACK, 128), BF16),
            image_scratch,
            interp_scratch,
            pltpu.SemaphoreType.DMA,
            *relay_sems(devices, pieces),
            *relay_sems(devices, 1),
        ],
        compiler_params=pltpu.CompilerParams(
            vmem_limit_bytes=VMEM_BYTES, collective_id=1, has_side_effects=True
        ),
        name="bend",
    )(
        block_corner,
        bend_planes,
        split,
        kern_high,
        kern_low,
        y_cell,
        box_row,
        probability,
        interp,
    )

    everything = totals[0] + totals[1] + totals[2]
    loglik = everything[:NTRIAL]
    descent = everything[NTRIAL : 2 * NTRIAL]
    quad_gu, quad_du, quad_dv = (everything[2 * NTRIAL + k] for k in range(3))
    prior = 0.5 * (quad_gu + 2.0 * trial_steps * quad_du + trial_steps * trial_steps * quad_dv)
    trial_objective = (loglik - prior) / points
    trial_slope = (descent - quad_du - trial_steps * quad_dv) / points
    return (new_weights, grid_gradient, curvature, trial_objective, trial_slope)


def solution(mesh):
    return jax.shard_map(
        body,
        mesh=mesh,
        in_specs=(
            P(("parts", "pts"), None, None),
            P(("parts", "pts"), None, None),
            P(),
            P(),
            P(),
            P(("parts", "pts"), None, None),
            P(None, ("parts", "pts")),
            P(("parts", "pts"), None),
            P(("parts", "pts"), None),
            P(),
            P(),
        ),
        out_specs=(
            P(("parts", "pts"), None, None),
            P(("parts", "pts"), None, None),
            P(("parts", "pts"), None),
            P("parts"),
            P("parts"),
        ),
        check_vma=False,
    )
```

profile of v0, /device:TPU:0, one launch (start us, length us, event | category | flops | bytes accessed | tf_op | source)
XLA Modules:
  0.0 222.5 jit_solution(561478784553034703)
XLA Ops:
  0.7 0.7 slice_bitcast_fusion
  1.4 1.9 fusion.18
  3.3 0.9 copy.24
  4.6 0.7 fusion.14
  5.4 0.6 pad_add_fusion.offs_ref
  6.7 0.6 fusion.39
  7.3 0.6 fusion.30
  8.5 0.9 copy.22
  9.4 0.6 fusion.28
  10.6 0.9 copy.23
  11.4 1.0 copy.27
  12.4 1.0 copy.28
  13.4 109.5 %forward.1 = (f32[128,128]{1,0:T(8,128)}, f32[8,128]{1,0:T(8,128)}, s16[16,144,256]{2,1,0:T(8,128)(2,1)}, bf16[16,128,256]{2,1,0:T(8,128)(2,1)}) custom-call(s32[3,128]{1,0:T(4,128)} %corner_ref.3, f32[1]{0:T(128)} %bitcast.1.chosen_ref, f32[5]{0:T(128)} %trial_ref.1, bf16[64,16,128]{2,1,0:T(8,128)(2,1)} %bitcast.76, bf16[64,16,128]{2,1,0:T(8,128)(2,1)} %bitcast.77, ...), custom_call_target="tpu_custom_call" | custom-call | tf_op jit(solution)/shard_map/forward/pallas_call | solution.py:534
  122.9 0.8 slice_convert_fusion
  123.7 1.3 fusion.42
  125.0 1.3 slice.57
  126.3 5.7 %fusion.10 = (s32[2048,256]{1,0:T(8,128)}, s32[2048,256]{1,0:T(8,128)}) fusion(s16[16,128,256]{2,1,0:T(8,128)(2,1)S(1)} %slice.57, s32[2048]{0:T(1024)S(1)} %bitcast.79, s32[2048]{0:T(1024)S(1)} %bitcast.82), kind=kLoop, calls=%fused_computation.24 | loop fusion | flops 25690112 | bytes 5259264 | tf_op jit(solution)/shard_map/jit(_where)/select_n | solution.py:589
  132.0 5.0 %sort.14 = (s32[2048]{0:T(1024)S(1)}, s32[2048]{0:T(1024)}) sort(s32[2048]{0:T(1024)S(1)} %add_select_fusion.8, s32[2048]{0:T(1024)S(1)} %iota.30), dimensions={0}, to_apply=%region_1.2 | sort | flops 22528 | bytes 32768 | tf_op jit(solution)/shard_map/sort | solution.py:594
  137.0 0.6 compare_select_fusion.ids_ref
  137.6 1.5 bitcast_convert_fusion.term_ref
  139.2 11.9 %spread.1 = f32[1024,128]{1,0:T(8,128)} custom-call(s32[2048]{0:T(1024)} %compare_select_fusion.ids_ref, s32[1]{0:T(128)} %bitcast.11.count_ref, s32[2048]{0:T(1024)} %bitcast.81, s32[2048,256]{1,0:T(8,128)} %get-tuple-element.25.y_ref, s32[2048,256]{1,0:T(8,128)} %get-tuple-element.24.key_ref, f32[2048,256]{1,0:T(8,128)} %bitcast_convert_fusion.term_ref), custom_call_target="tpu_custom_call" | custom-call | tf_op jit(solution)/shard_map/spread/pallas_call | solution.py:598
  151.1 1.2 copy.29
  152.3 1.5 bitcast_subtract_fusion
  153.9 0.6 convolution_bitcast_fusion
  155.1 0.9 copy.30
  155.9 0.7 reduce-precision_convert_fusion.2
  156.6 0.6 fusion.37.split_ref
  157.2 59.1 %bend.1 = (f32[128,128]{1,0:T(8,128)}, f32[16,128]{1,0:T(8,128)}) custom-call(s32[3,128]{1,0:T(4,128)} %corner_ref.3, bf16[64,16,128]{2,1,0:T(8,128)(2,1)} %bitcast.73, bf16[16,128]{1,0:T(8,128)(2,1)} %fusion.37.split_ref, bf16[256,256]{1,0:T(8,128)(2,1)} %get-tuple-element.27.kh_ref, bf16[256,256]{1,0:T(8,128)(2,1)} %get-tuple-element.26.kl_ref, ...), custom_call_target="tpu_custom_call" | custom-call | tf_op jit(solution)/shard_map/bend/pallas_call | solution.py:625
  216.4 0.8 slice_add_fusion
  217.2 0.7 fusion.43
  218.5 2.5 %fusion.40 = (f32[5]{0:T(128)}, f32[5]{0:T(128)}) fusion(f32[5]{0:T(128)S(1)} %copy-done.8, f32[1,128]{1,0:T(1,128)S(1)} %slice_add_fusion, f32[]{:T(128)} %bitcast.23, f32[]{:T(128)} %bitcast.24, f32[]{:T(128)S(6)} %mul.72, f32[]{:T(128)} %bitcast.22), kind=kLoop, calls=%fused_computation.91 | loop fusion | flops 60 | bytes 116 | tf_op jit(solution)/shard_map/div | solution.py:661
  221.0 1.5 copy.36
  (28 shorter events, 2.1 us)
Async XLA Ops:
  0.6 6.6 %copy-start = (f32[128,128]{1,0:T(8,128)S(1)}, f32[128,128]{1,0:T(8,128)}, u32[]{:S(2)}) copy-start(f32[128,128]{1,0:T(8,128)} %param.15) | copy-start | bytes 196612
  0.6 4.7 %copy-start.6 = (s32[3,128]{1,0:T(4,128)S(1)}, s32[3,128]{1,0:T(4,128)}, u32[]{:S(2)}) copy-start(s32[3,128]{1,0:T(4,128)} %corner_ref.3) | copy-start | bytes 4612
  0.7 6.0 %copy-start.7 = (f32[5]{0:T(128)S(1)}, f32[5]{0:T(128)}, u32[]{:S(2)}) copy-start(f32[5]{0:T(128)} %trial_ref.1) | copy-start | bytes 64
  0.7 6.6 %copy-start.1 = (f32[8,128,128]{2,1,0:T(8,128)S(1)}, f32[8,128,128]{2,1,0:T(8,128)}, u32[]{:S(2)}) copy-start(f32[8,128,128]{2,1,0:T(8,128)} %param.11) | copy-start | bytes 1572868
  0.7 7.2 %copy-start.5 = (f32[128,128]{1,0:T(8,128)S(1)}, f32[128,128]{1,0:T(8,128)}, u32[]{:S(2)}) copy-start(f32[128,128]{1,0:T(8,128)} %param.14) | copy-start | bytes 196612
  4.4 4.9 %copy-start.2 = (f32[8,128,128]{2,1,0:T(8,128)S(1)}, f32[8,128,128]{2,1,0:T(8,128)}, u32[]{:S(2)}) copy-start(f32[8,128,128]{2,1,0:T(8,128)} %param.12) | copy-start | bytes 1572868
  126.3 11.3 %copy-start.4 = (bf16[16,128,256]{2,1,0:T(8,128)(2,1)S(1)}, bf16[16,128,256]{2,1,0:T(8,128)(2,1)}, u32[]{:S(2)}) copy-start(bf16[16,128,256]{2,1,0:T(8,128)(2,1)} %get-tuple-element.15) | copy-start | bytes 3145732
  153.9 62.5 %copy-start.3 = (f32[8,128,128]{2,1,0:T(8,128)}, f32[8,128,128]{2,1,0:T(8,128)S(1)}, u32[]{:S(2)}) copy-start(f32[8,128,128]{2,1,0:T(8,128)S(1)} %get-tuple-element.49) | copy-start | bytes 1572868
  157.2 61.3 %copy-start.8 = (f32[5]{0:T(128)S(1)}, f32[5]{0:T(128)}, u32[]{:S(2)}) copy-start(f32[5]{0:T(128)} %trial_ref.1) | copy-start | bytes 64
where the time goes:
time: 224 us; the launch traced here: 222 us
  Pallas kernels  181 us (81%)
  other arithmetic  25 us (11%)
  local copies, waits for them, and re-layouts  11.2 us (5%)
  matrix products  3.53 us (2%)
    pallas_call x1, Pallas kernels, body(): pl.pallas_call(functools.partial(forward_kernel, group), in_specs=[smem]...  110 us
    pallas_call x1, Pallas kernels, body(): pl.pallas_call(functools.partial(bend_kernel, group), in_specs=[smem] + [...  59.1 us
    pallas_call x1, Pallas kernels, body(): pl.pallas_call(functools.partial(scatter_kernel, slab, unroll), grid_spec...  11.9 us
    select_n x1, other arithmetic, body(): key = jnp.where(inside, far_offsets % BOXZ * slab + far_cell, -1)  5.68 us
    sort x1, other arithmetic, body(): ids = lax.sort(jnp.where(touches, ranks, ranks + total))  5.04 us

commit v1 on v0

v1 whole, which is shorter than its diff:
```python
import functools

import jax
import jax.numpy as jnp
from jax import lax
from jax.experimental import pallas as pl
from jax.experimental.pallas import tpu as pltpu
from jax.sharding import PartitionSpec as P

BOXX = 16
BOXY = 16
BOXZ = 8
NTRIAL = 5
PACK = 16
VMEM_BYTES = 62 * 1024 * 1024
UP, DOWN, SIDE, TWIN = range(4)

HIGHEST = lax.Precision.HIGHEST
F32 = jnp.float32
BF16 = jnp.bfloat16
NT = (((1,), (1,)), ((), ()))
MESH = pl.DeviceIdType.MESH


def high_part(value):
    return lax.reduce_precision(value, 8, 7)


def widen_kern(kern_x, devices, slab, group):
    size_x = kern_x.shape[0]
    parts = kern_x.reshape(1, size_x, devices, 1, slab)
    same = jnp.eye(group, dtype=F32).reshape(group, 1, 1, group, 1)
    wide = (parts * same).reshape(group * size_x, devices * group * slab)
    high = high_part(wide)
    return high.astype(BF16), (wide - high).astype(BF16)


class Place:
    def __init__(self, devices):
        me = lax.axis_index("pts")
        self.devices = devices
        self.depths = devices // 4
        self.me = me
        self.core = lax.rem(me, 2)
        self.side = lax.rem(lax.div(me, 2), 2)
        self.depth = lax.div(me, 4)

    def slot(self, depth, side, core):
        return (depth * 2 + side) * 2 + core

    def target(self, kind):
        if kind == UP:
            return self.slot(self.depth + 1, self.side, self.core)
        if kind == DOWN:
            return self.slot(self.depth - 1, self.side, self.core)
        if kind == SIDE:
            return self.slot(self.depth, 1 - self.side, self.core)
        return self.slot(self.depth, self.side, 1 - self.core)

    def greet(self):
        barrier = pltpu.get_barrier_semaphore()

        def tell(kind):
            pl.semaphore_signal(
                barrier, inc=1, device_id={"pts": self.target(kind)}, device_id_type=MESH
            )

        tell(SIDE)
        tell(TWIN)

        @pl.when(self.depth + 1 < self.depths)
        def _():
            tell(UP)

        @pl.when(self.depth > 0)
        def _():
            tell(DOWN)

        above = jnp.where(self.depth + 1 < self.depths, 1, 0)
        below = jnp.where(self.depth > 0, 1, 0)
        pl.semaphore_wait(barrier, 2 + above + below)


class Relay:
    def __init__(self, place, own, buf, send, recv):
        self.place = place
        self.own = own
        self.buf = buf
        self.send = send
        self.recv = recv
        self.pieces = recv.shape[1]
        self.size = own.shape[0] // self.pieces

    def copy(self, slot, piece, kind, mine=False):
        rows = pl.ds(piece * self.size, self.size)
        landing = self.buf.at[slot, rows]
        return pltpu.make_async_remote_copy(
            src_ref=self.own.at[rows] if mine else landing,
            dst_ref=landing,
            send_sem=self.send.at[kind, lax.div(slot, 2), piece],
            recv_sem=self.recv.at[slot, piece],
            device_id={"pts": self.place.target(kind)},
            device_id_type=MESH,
        )

    def take(self, slot, piece):
        self.copy(slot, piece, TWIN).wait_recv()

    def line_sends(self, depth, piece, act, mine=False):
        here = self.place
        slot = here.slot(depth, here.side, here.core)

        @pl.when((depth <= here.depth) & (here.depth + 1 < here.depths))
        def _():
            act(self.copy(slot, piece, UP, mine))

        @pl.when((depth >= here.depth) & (here.depth > 0))
        def _():
            act(self.copy(slot, piece, DOWN, mine))

        act(self.copy(slot, piece, SIDE, mine))
        act(self.copy(slot, piece, TWIN, mine))

    def side_sends(self, depth, piece, act):
        here = self.place
        act(self.copy(here.slot(depth, 1 - here.side, here.core), piece, TWIN))

    def start_own(self):
        def one(piece, carry):
            self.line_sends(self.place.depth, piece, lambda c: c.start(), mine=True)
            return carry

        lax.fori_loop(0, self.pieces, one, 0)

    def line_events(self, piece, far):
        here = self.place
        for way in (-1, 1):
            depth = here.depth + way * far

            @pl.when((far > 0) & (depth >= 0) & (depth < here.depths))
            def _():
                self.take(here.slot(depth, here.side, here.core), piece)
                self.line_sends(depth, piece, lambda c: c.start())

    def side_events(self, piece, far):
        here = self.place
        for way in (-1, 1):
            depth = here.depth + way * far
            wanted = (depth >= 0) & (depth < here.depths)
            if way > 0:
                wanted = wanted & (far > 0)

            @pl.when(wanted)
            def _():
                self.take(here.slot(depth, 1 - here.side, here.core), piece)
                self.side_sends(depth, piece, lambda c: c.start())

    def twin_events(self, piece):
        here = self.place

        def one(pair, carry):
            self.take(pair * 2 + (1 - here.core), piece)
            return carry

        lax.fori_loop(0, here.devices // 2, one, 0)

    def run(self, work=None, steps=0, mix=None, tail=None, riders=()):
        depths, pieces = self.place.depths, self.pieces

        def one(wave, carry):
            def near(far, carry):
                piece = wave - far

                @pl.when((piece >= 0) & (piece < pieces))
                def _():
                    self.line_events(piece, far)

                @pl.when((piece >= 1) & (piece < pieces + 1))
                def _():
                    self.side_events(piece - 1, far)

                for rider in riders:

                    @pl.when(piece == 0)
                    def _():
                        rider.line_events(0, far)

                    @pl.when(piece == 1)
                    def _():
                        rider.side_events(0, far)

                return carry

            lax.fori_loop(0, depths, near, 0)
            if tail is not None:

                @pl.when(wave == pieces + depths - 2)
                def _():
                    tail()

            if work is not None:

                @pl.when(wave < steps)
                def _():
                    work(wave)

            full = wave - depths - 1

            @pl.when(full >= 0)
            def _():
                self.twin_events(full)
                if mix is not None:
                    mix(full)

            for rider in riders:

                @pl.when(full == 0)
                def _():
                    rider.twin_events(0)

            return carry

        lax.fori_loop(0, pieces + depths + 1, one, 0)

    def finish(self):
        def one(step, carry):
            piece = lax.div(step, self.place.depths)
            depth = lax.rem(step, self.place.depths)
            self.line_sends(depth, piece, lambda c: c.wait_send())
            self.side_sends(depth, piece, lambda c: c.wait_send())
            return carry

        lax.fori_loop(0, self.pieces * self.place.depths, one, 0)


def relay_sems(devices, pieces):
    return [
        pltpu.SemaphoreType.DMA((4, devices // 2, pieces)),
        pltpu.SemaphoreType.DMA((devices, pieces)),
    ]


def mix_depth(planes_ref, kh_ref, kl_ref, image, group, size_x, first, count):
    devices, _, pack, lanes = planes_ref.shape

    def one(step, carry):
        at = first + step * 2
        pair = [planes_ref[:, at + t].reshape(devices * pack, lanes) for t in range(2)]
        rhs = jnp.concatenate(pair, axis=1)
        mixed = jnp.dot(kh_ref[...], rhs, preferred_element_type=F32)
        mixed = mixed + jnp.dot(kl_ref[...], rhs, preferred_element_type=F32)
        for t in range(2):
            for g in range(group):
                image[(at + t) * group + g] = mixed[
                    g * size_x : (g + 1) * size_x, t * lanes : (t + 1) * lanes
                ]
        return carry

    lax.fori_loop(0, count // 2, one, 0)


def split_offset(offset):
    bits_y, bits_z = BOXY.bit_length() - 1, BOXZ.bit_length() - 1
    return offset >> (bits_y + bits_z), (offset >> bits_z) & (BOXY - 1), offset & (BOXZ - 1)


def pick_values(image, corner_ref, offsets_ref, block):
    size_y = image.shape[-1]
    cols = offsets_ref.shape[-1]
    box_rows = BOXZ * BOXX
    at_x, at_y, at_z = (corner_ref[k, block] for k in range(3))
    off_x, off_y, off_z = split_offset(offsets_ref[pl.ds(block, 1), :])
    y_cell = at_y + off_y
    box_row = off_z * BOXX + off_x
    box = image[pl.ds(at_z, BOXZ), pl.ds(at_x, BOXX), :]
    box = box.reshape(box_rows, size_y).astype(BF16)
    y_line = lax.broadcasted_iota(jnp.int32, (size_y, cols), 0)
    pick_y = jnp.where(y_line == y_cell, 1.0, 0.0).astype(BF16)
    lines = jnp.dot(box, pick_y, preferred_element_type=F32)
    row_line = lax.broadcasted_iota(jnp.int32, (box_rows, cols), 0)
    line = jnp.where(row_line == box_row, lines, 0.0)
    value = jnp.sum(line, axis=0, keepdims=True)
    return jnp.broadcast_to(value, (8, cols)).astype(BF16)


def interpolate_blocks(image, corner_ref, offsets_ref, interp, out_ref, first, count):
    unroll = min(16, count)

    def some(part, carry):
        for k in range(unroll):
            block = first + part * unroll + k
            values = pick_values(image, corner_ref, offsets_ref, block)
            line = lax.dot_general(values, interp[block], NT, preferred_element_type=F32)
            out_ref[pl.ds(block, 1), :] = line[0:1]
        return carry

    lax.fori_loop(0, count // unroll, some, 0)


def power_below(value):
    return 1 << (value.bit_length() - 1)


def mix_planes(field_of, kern_y_ref, kern_z_ref, rows, planes_ref, slab):
    size_z = kern_z_ref.shape[0]
    for x in range(slab):
        inner = lax.dot_general(
            kern_z_ref[...], field_of(x), NT, precision=HIGHEST, preferred_element_type=F32
        )
        plane = lax.dot_general(
            inner, kern_y_ref[...], NT, precision=HIGHEST, preferred_element_type=F32
        )
        rows[pl.ds(x, size_z, stride=slab), :] = plane
    planes_ref[...] = rows[...].astype(BF16).reshape(planes_ref.shape)


def planes_kernel(weights_ref, direction_ref, kern_y_ref, kern_z_ref, out_u, out_d, rows):
    slab = weights_ref.shape[0]
    mix_planes(lambda x: weights_ref[x], kern_y_ref, kern_z_ref, rows, out_u, slab)
    mix_planes(lambda x: direction_ref[x], kern_y_ref, kern_z_ref, rows, out_d, slab)


def rank_blocks(corners, me, slab, ranks_ref, list_ref):
    devices, blocks = corners.shape
    from_x = (corners & 255) - me * slab
    touch = jnp.where((from_x < slab) & (from_x > -BOXX), 1.0, 0.0)
    earlier = lax.broadcasted_iota(jnp.int32, (blocks, blocks), 0)
    earlier = earlier < lax.broadcasted_iota(jnp.int32, (blocks, blocks), 1)
    within = jnp.dot(
        touch.astype(BF16), jnp.where(earlier, 1.0, 0.0).astype(BF16), preferred_element_type=F32
    )
    count = jnp.sum(touch, axis=1, keepdims=True)
    below = lax.broadcasted_iota(jnp.int32, (devices, devices), 1)
    below = below < lax.broadcasted_iota(jnp.int32, (devices, devices), 0)
    base = jnp.dot(
        jnp.where(below, 1.0, 0.0).astype(BF16),
        jnp.broadcast_to(count, (devices, blocks)).astype(BF16),
        preferred_element_type=F32,
    )
    ranks = jnp.where(touch > 0.0, base + within, -1.0)
    for device in range(devices):
        line = jnp.broadcast_to(ranks[device : device + 1], (blocks, blocks))
        ranks_ref[device] = jnp.transpose(line)
    total = jnp.sum(touch)
    list_ref[pl.ds(devices, 8), :] = jnp.full((8, blocks), total, F32).astype(jnp.int32)


def list_blocks(ranks_ref, list_ref, line):
    devices, blocks, _ = ranks_ref.shape
    wanted = lax.broadcasted_iota(jnp.int32, (blocks, blocks), 1) + line * blocks
    wanted = wanted.astype(F32)
    block = lax.broadcasted_iota(jnp.int32, (blocks, blocks), 0).astype(F32)

    def one(device, ids):
        hit = ranks_ref[device] == wanted
        start = (device * blocks).astype(F32)
        return ids + jnp.where(hit, block + start, 0.0)

    ids = lax.fori_loop(0, devices, one, jnp.zeros((blocks, blocks), F32))
    ids = jnp.sum(ids, axis=0, keepdims=True)
    list_ref[pl.ds(line, 1), :] = ids.astype(jnp.int32)


def log_sigmoid(value):
    return jnp.minimum(value, 0.0) - jnp.log1p(jnp.exp(-jnp.abs(value)))


def forward_kernel(
    group,
    corner_ref,
    trial_ref,
    accept_ref,
    own_u,
    own_d,
    packed_ref,
    kh_ref,
    kl_ref,
    offsets_ref,
    labels_ref,
    weights_ref,
    direction_ref,
    interp_ref,
    prob_ref,
    split_ref,
    list_ref,
    corners_ref,
    all_offs,
    all_terms,
    buf_u,
    buf_d,
    all_packed,
    image_u,
    image_d,
    interp,
    latent_ref,
    slope_ref,
    res_ref,
    term_ref,
    own_terms,
    own_offs,
    weights_t,
    direction_t,
    ranks_ref,
    local_sem,
    *sems,
):
    devices, units, pack, lanes = buf_u.shape
    blocks, per_block = labels_ref.shape
    slab = pack // group
    size_z, size_x, size_y = image_u.shape
    place = Place(devices)
    load = pltpu.make_async_copy(interp_ref, interp, local_sem)
    load.start()
    u = Relay(place, own_u, buf_u, sems[0], sems[1])
    d = Relay(place, own_d, buf_d, sems[2], sems[3])
    o = Relay(place, own_offs, all_offs, sems[4], sems[5])
    t = Relay(place, own_terms, all_terms, sems[6], sems[7])
    c = Relay(place, packed_ref, all_packed, sems[8], sems[9])
    place.greet()
    c.start_own()
    u.start_own()
    buf_u[place.me] = own_u[...]
    buf_d[place.me] = own_d[...]
    all_packed[place.me] = packed_ref[...]
    own_offs[...] = offsets_ref[...].astype(jnp.int16)
    all_offs[place.me] = own_offs[...]
    for x in range(slab):
        weights_t[pl.ds(x, size_z, stride=slab), :] = jnp.transpose(weights_ref[x])
        direction_t[pl.ds(x, size_z, stride=slab), :] = jnp.transpose(direction_ref[x])

    def mixer(buf, image):
        return lambda piece: mix_depth(
            buf, kh_ref, kl_ref, image, group, size_x, piece * u.size, u.size
        )

    u.run(mix=mixer(buf_u, image_u), tail=d.start_own, riders=(c,))
    corners = all_packed[:, 0, :]
    corners_ref[...] = corners
    rank_blocks(corners, place.me, slab, ranks_ref, list_ref)
    load.wait()
    steps = power_below(u.pieces + place.depths)
    some, lines = blocks // steps, -(-devices // steps)

    def early(step):
        interpolate_blocks(
            image_u, corner_ref, offsets_ref, interp, latent_ref, step * some, some
        )
        for k in range(lines):
            list_blocks(ranks_ref, list_ref, step * lines + k)

    d.run(work=early, steps=steps, mix=mixer(buf_d, image_d), tail=o.start_own)
    steps = power_below(place.depths)
    part = blocks // steps

    def late(step):
        interpolate_blocks(
            image_d, corner_ref, offsets_ref, interp, slope_ref, step * part, part
        )

    o.run(work=late, steps=steps)
    slope = slope_ref[...]
    latent = latent_ref[...]
    prob = jax.nn.sigmoid(latent + trial_ref[accept_ref[0]] * slope)
    prob_ref[...] = prob
    target = labels_ref[...].astype(F32)
    res_ref[...] = (target - prob).astype(BF16).astype(F32)
    unroll = 16

    def back(step, carry):
        for k in range(unroll):
            block = step * unroll + k
            row = jnp.broadcast_to(res_ref[pl.ds(block, 1), :], (8, per_block))
            term = jnp.dot(row.astype(BF16), interp[block], preferred_element_type=F32)
            term_ref[pl.ds(block, 1), :] = term[0:1]
        return carry

    lax.fori_loop(0, blocks // unroll, back, 0)
    own_terms[...] = term_ref[...].astype(BF16)
    all_terms[place.me] = own_terms[...]
    for relay in (c, u, d, o):
        relay.finish()
    at = pl.multiple_of(place.me * slab, slab)
    image_w = image_u[:, pl.ds(at, slab), :]
    image_t = image_d[:, pl.ds(at, slab), :]
    weights_rows = weights_t[...].reshape(size_z, slab, size_y)
    direction_rows = direction_t[...].reshape(size_z, slab, size_y)
    sums = [
        jnp.sum(weights_rows * image_w),
        jnp.sum(direction_rows * image_w),
        jnp.sum(direction_rows * image_t),
    ]
    t.start_own()
    signed = 2.0 * target - 1.0
    loglik, descent = [], []
    for k in range(NTRIAL):
        at_trial = latent + trial_ref[k] * slope
        loglik.append(jnp.sum(log_sigmoid(signed * at_trial)))
        descent.append(jnp.sum((target - jax.nn.sigmoid(at_trial)) * slope))
    lane = lax.broadcasted_iota(jnp.int32, split_ref.shape, 1)
    row = jnp.zeros(split_ref.shape, F32)
    for k, value in enumerate(loglik + descent + sums):
        row = jnp.where(lane == k, value, row)
    first = row.astype(BF16).astype(F32)
    second = (row - first).astype(BF16).astype(F32)
    third = row - first - second
    line = lax.broadcasted_iota(jnp.int32, split_ref.shape, 0)
    split = jnp.where(line == 0, first, jnp.where(line == 1, second, third))
    split_ref[...] = jnp.where(line < 3, split, 0.0).astype(BF16)
    t.run()
    t.finish()


def bend_kernel(
    group,
    corner_ref,
    own_ref,
    split_ref,
    kh_ref,
    kl_ref,
    offsets_ref,
    prob_ref,
    interp_ref,
    out_ref,
    total_ref,
    buf,
    all_split,
    image,
    interp,
    local_sem,
    *sems,
):
    devices = buf.shape[0]
    blocks = prob_ref.shape[0]
    size_x = image.shape[1]
    place = Place(devices)
    load = pltpu.make_async_copy(interp_ref, interp, local_sem)
    load.start()
    b = Relay(place, own_ref, buf, sems[0], sems[1])
    s = Relay(place, split_ref, all_split, sems[2], sems[3])
    place.greet()
    s.start_own()
    b.start_own()
    buf[place.me] = own_ref[...]
    all_split[place.me] = split_ref[...]
    b.run(
        mix=lambda piece: mix_depth(
            buf, kh_ref, kl_ref, image, group, size_x, piece * b.size, b.size
        ),
        riders=(s,),
    )
    load.wait()
    total = jnp.sum(all_split[...].astype(F32), axis=0)
    total_ref[...] = total[0:1] + total[1:2] + total[2:3]
    interpolate_blocks(image, corner_ref, offsets_ref, interp, out_ref, 0, blocks)
    prob = prob_ref[...]
    out_ref[...] = prob * (1.0 - prob) * out_ref[...]
    b.finish()
    s.finish()


def spread_kernel(
    list_ref,
    corners_ref,
    trial_ref,
    accept_ref,
    offs_ref,
    terms_ref,
    weights_ref,
    direction_ref,
    kern_y_ref,
    kern_z_ref,
    new_ref,
    grad_ref,
    planes_ref,
    offs,
    terms,
    spread,
):
    devices, blocks, cols = offs_ref.shape
    slab, size_y, size_z = weights_ref.shape
    rows = BOXZ * slab
    unroll = 8
    me = lax.axis_index("pts")
    spread[...] = jnp.zeros_like(spread)

    def widen(device, carry):
        offs[pl.ds(pl.multiple_of(device * blocks, blocks), blocks)] = offs_ref[device].astype(
            jnp.int32
        )
        terms[pl.ds(pl.multiple_of(device * blocks, blocks), blocks)] = terms_ref[device].astype(
            F32
        )
        return carry

    lax.fori_loop(0, devices, widen, 0)
    count = list_ref[devices, 0]

    def some(part, carry):
        sums = []
        for k in range(unroll):
            at = part * unroll + k
            block = list_ref[lax.div(at, blocks), lax.rem(at, blocks)]
            packed = corners_ref[lax.div(block, blocks), lax.rem(block, blocks)]
            from_x = jnp.where(at < count, (packed & 255) - me * slab, -2 * BOXX)
            at_y = (packed >> 8) & 255
            at_z = packed >> 16
            off_x, off_y, off_z = split_offset(offs[pl.ds(block, 1), :])
            cell = off_x + from_x
            key = jnp.where((cell >= 0) & (cell < slab), off_z * slab + cell, -1)
            y_cell = off_y + at_y
            row_line = lax.broadcasted_iota(jnp.int32, (rows, cols), 0)
            y_line = lax.broadcasted_iota(jnp.int32, (size_y, cols), 0)
            left = jnp.where(row_line == key, terms[pl.ds(block, 1), :], 0.0).astype(BF16)
            right = jnp.where(y_line == y_cell, 1.0, 0.0).astype(BF16)
            sums.append((at_z, lax.dot_general(left, right, NT, preferred_element_type=F32)))
        for at_z, piece in sums:
            spread[pl.ds(pl.multiple_of(at_z * slab, slab), rows), :] += piece
        return carry

    lax.fori_loop(0, lax.div(count + unroll - 1, unroll), some, 0)
    chosen = trial_ref[accept_ref[0]]
    for x in range(slab):
        new = weights_ref[x] + chosen * direction_ref[x]
        new_ref[x] = new
        grad_ref[x] = jnp.transpose(spread[pl.ds(x, size_z, stride=slab), :]) - new
    mix_planes(lambda x: grad_ref[x], kern_y_ref, kern_z_ref, spread, planes_ref, slab)


def body(
    grid_weights,
    direction,
    kern_x,
    kern_y,
    kern_z,
    interp,
    block_corner,
    block_offsets,
    labels,
    trial_steps,
    accept,
):
    slab, size_y, size_z = grid_weights.shape
    size_x = kern_x.shape[0]
    devices = lax.axis_size("pts")
    blocks, cols = block_offsets.shape
    per_block = interp.shape[1]
    points = blocks * per_block * devices
    group = max(1, PACK // slab)
    pack = group * slab
    units = size_z // group
    pieces = max(1, 64 // devices)

    packed = block_corner[0] + block_corner[1] * 256 + block_corner[2] * 65536
    packed = jnp.broadcast_to(packed[None], (8, blocks))
    kern_high, kern_low = widen_kern(kern_x, devices, slab, group)

    smem = pl.BlockSpec(memory_space=pltpu.SMEM)
    vmem = pl.BlockSpec(memory_space=pltpu.VMEM)
    hbm = pl.BlockSpec(memory_space=pl.ANY)
    limit = dict(vmem_limit_bytes=VMEM_BYTES)
    planes_shape = jax.ShapeDtypeStruct((units, pack, size_y), BF16)
    rows_scratch = pltpu.VMEM((size_z * slab, size_y), F32)
    planes_scratch = pltpu.VMEM((devices, units, pack, size_y), BF16)
    image_scratch = pltpu.VMEM((size_z, size_x, size_y), F32)
    interp_scratch = pltpu.VMEM(interp.shape, BF16)
    point_scratch = pltpu.VMEM((blocks, per_block), F32)
    point_shape = jax.ShapeDtypeStruct((blocks, per_block), F32)

    planes_w, planes_d = pl.pallas_call(
        planes_kernel,
        in_specs=[vmem] * 4,
        out_specs=[vmem] * 2,
        out_shape=[planes_shape] * 2,
        scratch_shapes=[rows_scratch],
        compiler_params=pltpu.CompilerParams(**limit),
        name="planes",
    )(grid_weights, direction, kern_y, kern_z)

    probability, split, block_list, corners, offsets, terms = pl.pallas_call(
        functools.partial(forward_kernel, group),
        in_specs=[smem] * 3 + [vmem] * 9 + [hbm],
        out_specs=[vmem] * 6,
        out_shape=[
            point_shape,
            jax.ShapeDtypeStruct((PACK, 128), BF16),
            jax.ShapeDtypeStruct((devices + 8, blocks), jnp.int32),
            jax.ShapeDtypeStruct((devices, blocks), jnp.int32),
            jax.ShapeDtypeStruct((devices, blocks, cols), jnp.int16),
            jax.ShapeDtypeStruct((devices, blocks, cols), BF16),
        ],
        scratch_shapes=[
            planes_scratch,
            planes_scratch,
            pltpu.VMEM((devices, 8, blocks), jnp.int32),
            image_scratch,
            image_scratch,
            interp_scratch,
            point_scratch,
            point_scratch,
            point_scratch,
            pltpu.VMEM((blocks, cols), F32),
            pltpu.VMEM((blocks, cols), BF16),
            pltpu.VMEM((blocks, cols), jnp.int16),
            rows_scratch,
            rows_scratch,
            pltpu.VMEM((devices, blocks, blocks), F32),
            pltpu.SemaphoreType.DMA,
            *relay_sems(devices, pieces),
            *relay_sems(devices, pieces),
            *relay_sems(devices, 1),
            *relay_sems(devices, 1),
            *relay_sems(devices, 1),
        ],
        compiler_params=pltpu.CompilerParams(collective_id=0, has_side_effects=True, **limit),
        name="forward",
    )(
        block_corner,
        trial_steps,
        accept,
        planes_w,
        planes_d,
        packed,
        kern_high,
        kern_low,
        block_offsets,
        labels,
        grid_weights,
        direction,
        interp,
    )

    new_weights, grid_gradient, bend_planes = pl.pallas_call(
        spread_kernel,
        in_specs=[smem] * 4 + [vmem] * 6,
        out_specs=[vmem] * 3,
        out_shape=[
            jax.ShapeDtypeStruct(grid_weights.shape, F32),
            jax.ShapeDtypeStruct(grid_weights.shape, F32),
            planes_shape,
        ],
        scratch_shapes=[
            pltpu.VMEM((devices * blocks, cols), jnp.int32),
            pltpu.VMEM((devices * blocks, cols), F32),
            rows_scratch,
        ],
        compiler_params=pltpu.CompilerParams(**limit),
        name="spread",
    )(
        block_list,
        corners,
        trial_steps,
        accept,
        offsets,
        terms,
        grid_weights,
        direction,
        kern_y,
        kern_z,
    )

    curvature, totals = pl.pallas_call(
        functools.partial(bend_kernel, group),
        in_specs=[smem] + [vmem] * 6 + [hbm],
        out_specs=[vmem] * 2,
        out_shape=[point_shape, jax.ShapeDtypeStruct((1, 128), F32)],
        scratch_shapes=[
            planes_scratch,
            pltpu.VMEM((devices, PACK, 128), BF16),
            image_scratch,
            interp_scratch,
            pltpu.SemaphoreType.DMA,
            *relay_sems(devices, pieces),
            *relay_sems(devices, 1),
        ],
        compiler_params=pltpu.CompilerParams(collective_id=1, has_side_effects=True, **limit),
        name="bend",
    )(
        block_corner,
        bend_planes,
        split,
        kern_high,
        kern_low,
        block_offsets,
        probability,
        interp,
    )

    everything = totals[0]
    loglik = everything[:NTRIAL]
    descent = everything[NTRIAL : 2 * NTRIAL]
    quad_gu, quad_du, quad_dv = (everything[2 * NTRIAL + k] for k in range(3))
    prior = 0.5 * (quad_gu + 2.0 * trial_steps * quad_du + trial_steps * trial_steps * quad_dv)
    trial_objective = (loglik - prior) / points
    trial_slope = (descent - quad_du - trial_steps * quad_dv) / points
    return (new_weights, grid_gradient, curvature, trial_objective, trial_slope)


def solution(mesh):
    return jax.shard_map(
        body,
        mesh=mesh,
        in_specs=(
            P(("parts", "pts"), None, None),
            P(("parts", "pts"), None, None),
            P(),
            P(),
            P(),
            P(("parts", "pts"), None, None),
            P(None, ("parts", "pts")),
            P(("parts", "pts"), None),
            P(("parts", "pts"), None),
            P(),
            P(),
        ),
        out_specs=(
            P(("parts", "pts"), None, None),
            P(("parts", "pts"), None, None),
            P(("parts", "pts"), None),
            P("parts"),
            P("parts"),
        ),
        check_vma=False,
    )
```

time: 224 us -> 191 us (0.85)
  other arithmetic: 25 us -> 4.92 us
  local copies, waits for them, and re-layouts: 11.2 us -> 4.54 us
  matrix products: 3.53 us -> 0 us
    select_n x3 -> x0, other arithmetic: 6.28 us -> none  [the longest x1 5.68 us: body(): key = jnp.where(inside, far_offsets % BOXZ * slab + far_cell, -1)]
    sort x1 -> x0, other arithmetic: 5.04 us -> none  [body(): ids = lax.sort(jnp.where(touches, ranks, ranks + total))]
    pallas_call x1, Pallas kernels: 59.1 us -> 54.7 us  [body(): pl.pallas_call(functools.partial(bend_kernel, group), in_specs=[smem] + [...]
    pallas_call x1 -> x2, Pallas kernels: 11.9 us -> 16.3 us  [the longest x1 10.6 us: body(): pl.pallas_call(spread_kernel, in_specs=[smem] * 4 + [vmem] * 6, out_specs...]
    dot_general x6 -> x0, matrix products: 3.53 us -> none  [the longest x3 1.78 us: plane_mix(): inner = jnp.einsum('zc,fabc->zfab', kern_z, fields_zc, precision=HIGHEST)]
    add x2 -> x0, other arithmetic: 2.69 us -> none  [the longest x1 1.89 us: body(): box_row = block_offsets % BOXZ * BOXX + block_offsets // (BOXY * BOXZ)]
    convert_element_type x3 -> x0, local copies, waits for them, and re-layouts: 2.63 us -> none  [plane_mix(): jnp.einsum('zfab,yb->zfay', inner, kern_y, precision=HIGHEST).astype(BF16)]
    convert_element_type x2 -> x0, other arithmetic: 2.31 us -> none  [the longest x1 1.55 us: body(): terms = terms.reshape(devices * blocks, cols).astype(F32)]
where the time goes in v1:
time: 191 us; the launch traced here: 190 us
  Pallas kernels  179 us (94%)
  other arithmetic  4.92 us (3%)
  local copies, waits for them, and re-layouts  4.54 us (2%)
  between operations  1.99 us (1%)
    pallas_call x1, Pallas kernels, body(): pl.pallas_call(functools.partial(forward_kernel, group), in_specs=[smem]...  108 us
    pallas_call x1, Pallas kernels, body(): pl.pallas_call(functools.partial(bend_kernel, group), in_specs=[smem] + [...  54.7 us
    pallas_call x1, Pallas kernels, body(): pl.pallas_call(spread_kernel, in_specs=[smem] * 4 + [vmem] * 6, out_specs...  10.6 us
    pallas_call x1, Pallas kernels, body(): pl.pallas_call(planes_kernel, in_specs=[vmem] * 4, out_specs=[vmem] * 2,...  5.68 us

profile of v1, /device:TPU:0, one launch (start us, length us, event | category | flops | bytes accessed | tf_op | source)
XLA Modules:
  0.0 190.0 jit_solution(15415587889474259754)
XLA Ops:
  1.3 0.8 add_bitcast_fusion
  2.1 0.6 broadcast_in_dim.9.packed_ref
  2.7 0.9 copy.16
  3.6 0.2 broadcast_multiply_fusion
  3.8 0.1 copy.17
  4.0 0.7 fusion
  4.7 5.7 %planes.1 = (bf16[64,16,128]{2,1,0:T(8,128)(2,1)}, bf16[64,16,128]{2,1,0:T(8,128)(2,1)}) custom-call(f32[8,128,128]{2,1,0:T(8,128)} %weights_ref.5, f32[8,128,128]{2,1,0:T(8,128)} %direction_ref.5, f32[128,128]{1,0:T(8,128)} %kern_y_ref.3, f32[128,128]{1,0:T(8,128)} %kern_z_ref.3), custom_call_target="tpu_custom_call" | custom-call | tf_op jit(solution)/shard_map/planes/pallas_call | solution.py:669
  10.4 107.6 %forward.1 = (f32[128,128]{1,0:T(8,128)}, bf16[16,128]{1,0:T(8,128)(2,1)}, s32[24,128]{1,0:T(8,128)}, s32[16,128]{1,0:T(8,128)}, s16[16,128,256]{2,1,0:T(8,128)(2,1)}, /*index=5*/bf16[16,128,256]{2,1,0:T(8,128)(2,1)}) custom-call(s32[3,128]{1,0:T(4,128)} %corner_ref.3, f32[5]{0:T(128)} %trial_ref.3, s32[1]{0:T(128)S(6)} %copy.23.accept_ref, ...), custom_call_target="tpu_custom_call" | custom-call | tf_op jit(solution)/shard_map/forward/pallas_call | solution.py:679
  118.0 0.0 copy-start
  118.0 10.6 %spread.1 = (f32[8,128,128]{2,1,0:T(8,128)}, f32[8,128,128]{2,1,0:T(8,128)}, bf16[64,16,128]{2,1,0:T(8,128)(2,1)}) custom-call(s32[24,128]{1,0:T(8,128)} %get-tuple-element.20.list_ref, s32[16,128]{1,0:T(8,128)} %get-tuple-element.21.corners_ref, f32[5]{0:T(128)} %trial_ref.3, s32[1]{0:T(128)S(6)} %copy.23.accept_ref, ...), custom_call_target="tpu_custom_call" | custom-call | tf_op jit(solution)/shard_map/spread/pallas_call | solution.py:732
  128.6 54.7 %bend.1 = (f32[128,128]{1,0:T(8,128)}, f32[1,128]{1,0:T(1,128)}) custom-call(s32[3,128]{1,0:T(4,128)} %corner_ref.3, bf16[64,16,128]{2,1,0:T(8,128)(2,1)} %get-tuple-element.26.own_ref, bf16[16,128]{1,0:T(8,128)(2,1)} %get-tuple-element.27.split_ref, bf16[256,256]{1,0:T(8,128)(2,1)} %get-tuple-element.32.kh_ref, bf16[256,256]{1,0:T(8,128)(2,1)} %get-tuple-element.31.kl_ref, ...), custom_call_target="tpu_custom_call" | custom-call | tf_op jit(solution)/shard_map/bend/pallas_call | solution.py:761
  183.3 1.4 fusion.3
  185.3 0.0 copy-done
  185.3 3.2 %fusion.1 = (f32[5]{0:T(128)}, f32[5]{0:T(128)}) fusion(f32[5]{0:T(128)S(1)} %copy-done, f32[1,128]{1,0:T(1,128)} %get-tuple-element.30, f32[]{:T(128)} %bitcast.4, f32[]{:T(128)} %bitcast.5, f32[]{:T(128)S(6)} %mul.69, f32[]{:T(128)} %bitcast.3), kind=kLoop, calls=%fused_computation.7 | loop fusion | flops 60 | bytes 116 | tf_op jit(solution)/shard_map/div | solution.py:794
  188.5 1.5 copy.24
  (2 shorter events, 0.0 us)
Async XLA Ops:
  118.0 67.4 %copy-start = (f32[5]{0:T(128)S(1)}, f32[5]{0:T(128)}, u32[]{:S(2)}) copy-start(f32[5]{0:T(128)} %trial_ref.3) | copy-start | bytes 64

commit v2 on v1

v2 whole, which is shorter than its diff:
```python
import functools

import jax
import jax.numpy as jnp
from jax import lax
from jax.experimental import pallas as pl
from jax.experimental.pallas import tpu as pltpu
from jax.sharding import PartitionSpec as P

BOXX = 16
BOXY = 16
BOXZ = 8
NTRIAL = 5
PACK = 16
VMEM_BYTES = 62 * 1024 * 1024

F32 = jnp.float32
BF16 = jnp.bfloat16
NT = (((1,), (1,)), ((), ()))
MESH = pl.DeviceIdType.MESH


class Place:
    def __init__(self, devices):
        me = lax.axis_index("pts")
        self.devices = devices
        self.depths = devices // 4
        self.me = me
        self.core = lax.rem(me, 2)
        self.side = lax.rem(lax.div(me, 2), 2)
        self.depth = lax.div(me, 4)
        self.half = lax.rem(self.depth, 2)
        self.beside = self.slot(self.depth, 1 - self.side, self.core)
        self.twin = self.slot(self.depth, self.side, 1 - self.core)
        self.mate = self.slot(self.depth + 1 - 2 * self.half, self.side, self.core)

    def slot(self, depth, side, core):
        return (depth * 2 + side) * 2 + core

    def along(self, depth):
        return self.slot(depth, self.side, self.core)

    def others(self, act):
        def one(far, carry):
            for way in (-1, 1):
                depth = self.depth + way * far

                @pl.when((depth >= 0) & (depth < self.depths))
                def _():
                    act(depth)

            return carry

        lax.fori_loop(1, self.depths, one, 0)

    def greet(self):
        barrier = pltpu.get_barrier_semaphore()

        def tell(device):
            pl.semaphore_signal(
                barrier, inc=1, device_id={"pts": device}, device_id_type=MESH
            )

        self.others(lambda depth: tell(self.along(depth)))
        tell(self.beside)
        tell(self.twin)
        pl.semaphore_wait(barrier, self.depths + 1)

    def push(self, source, landing, send_sem, recv_sem, device):
        return pltpu.make_async_remote_copy(
            src_ref=source,
            dst_ref=landing,
            send_sem=send_sem,
            recv_sem=recv_sem,
            device_id={"pts": device},
            device_id_type=MESH,
        )


class Relay:
    def __init__(self, place, own, buf, sems, halved=False):
        self.place = place
        self.own = own
        self.buf = buf
        self.line_sem, self.side_sem, self.twin_sem, self.recv = sems
        self.pieces = self.recv.shape[1]
        self.size = buf.shape[1] // self.pieces
        self.halved = halved

    def own_rows(self, piece, depth):
        first = piece * self.size
        if self.halved:
            first = first + lax.rem(depth, 2) * self.buf.shape[1]
        return self.own.at[pl.ds(first, self.size)]

    def landing(self, slot, piece):
        return self.buf.at[slot, pl.ds(piece * self.size, self.size)]

    def line_copy(self, piece, depth):
        here = self.place
        return here.push(
            self.own_rows(piece, depth),
            self.landing(here.me, piece),
            self.line_sem.at[depth, piece],
            self.recv.at[here.me, piece],
            here.along(depth),
        )

    def side_copy(self, piece, depth, mine=False):
        here = self.place
        slot = here.along(depth)
        landing = self.landing(slot, piece)
        return here.push(
            self.own_rows(piece, depth) if mine else landing,
            landing,
            self.side_sem.at[depth, piece],
            self.recv.at[slot, piece],
            here.beside,
        )

    def twin_copy(self, piece, depth, side, mine=False):
        here = self.place
        slot = here.slot(depth, side, here.core)
        landing = self.landing(slot, piece)
        return here.push(
            self.own_rows(piece, depth) if mine else landing,
            landing,
            self.twin_sem.at[depth * 2 + side, piece],
            self.recv.at[slot, piece],
            here.twin,
        )

    def take(self, slot, piece):
        here = self.place
        landing = self.landing(slot, piece)
        here.push(
            landing, landing, self.twin_sem.at[0, piece], self.recv.at[slot, piece], here.twin
        ).wait_recv()

    def keep_own(self):
        here = self.place
        count = self.buf.shape[1]
        first = here.half * count if self.halved else 0
        self.buf[here.me] = self.own[pl.ds(first, count)]

    def start_own(self):
        here = self.place

        def one(piece, carry):
            here.others(lambda depth: self.line_copy(piece, depth).start())
            self.side_copy(piece, here.depth, mine=True).start()
            self.twin_copy(piece, here.depth, here.side, mine=True).start()
            return carry

        lax.fori_loop(0, self.pieces, one, 0)

    def line_events(self, piece):
        here = self.place

        def one(depth):
            self.take(here.along(depth), piece)
            self.side_copy(piece, depth).start()
            self.twin_copy(piece, depth, here.side).start()

        here.others(one)

    def side_events(self, piece):
        here = self.place

        def one(depth):
            self.take(here.slot(depth, 1 - here.side, here.core), piece)
            self.twin_copy(piece, depth, 1 - here.side).start()

        one(here.depth)
        here.others(one)

    def twin_events(self, piece):
        here = self.place

        def one(pair, carry):
            self.take(pair * 2 + (1 - here.core), piece)
            return carry

        lax.fori_loop(0, here.devices // 2, one, 0)

    def run(self, work=None, steps=0, mix=None, tail=None, riders=()):
        pieces = self.pieces

        def one(wave, carry):
            for rider in riders:

                @pl.when(wave == 0)
                def _():
                    rider.line_events(0)

                @pl.when(wave == 1)
                def _():
                    rider.side_events(0)

                @pl.when(wave == 2)
                def _():
                    rider.twin_events(0)

            @pl.when(wave < pieces)
            def _():
                self.line_events(wave)

            if tail is not None:

                @pl.when(wave == pieces - 1)
                def _():
                    tail()

            @pl.when((wave >= 1) & (wave < pieces + 1))
            def _():
                self.side_events(wave - 1)

            if work is not None:

                @pl.when(wave < steps)
                def _():
                    work(wave)

            @pl.when(wave >= 2)
            def _():
                self.twin_events(wave - 2)
                if mix is not None:
                    mix(wave - 2)

            return carry

        lax.fori_loop(0, pieces + 2, one, 0)

    def finish(self):
        here = self.place

        def one(step, carry):
            piece = lax.div(step, here.depths)
            depth = lax.rem(step, here.depths)

            @pl.when(depth != here.depth)
            def _():
                self.line_copy(piece, depth).wait_send()

            self.side_copy(piece, depth).wait_send()
            self.twin_copy(piece, depth, 0).wait_send()
            self.twin_copy(piece, depth, 1).wait_send()
            return carry

        lax.fori_loop(0, self.pieces * here.depths, one, 0)


def relay_sems(devices, pieces):
    depths = devices // 4
    return [
        pltpu.SemaphoreType.DMA((depths, pieces)),
        pltpu.SemaphoreType.DMA((depths, pieces)),
        pltpu.SemaphoreType.DMA((depths * 2, pieces)),
        pltpu.SemaphoreType.DMA((devices, pieces)),
    ]


def mix_depth(planes_ref, kh_ref, kl_ref, image, group, size_x, first, count):
    devices, _, pack, lanes = planes_ref.shape

    def one(step, carry):
        at = first + step * 2
        pair = [planes_ref[:, at + t].reshape(devices * pack, lanes) for t in range(2)]
        rhs = jnp.concatenate(pair, axis=1)
        mixed = jnp.dot(kh_ref[...], rhs, preferred_element_type=F32)
        mixed = mixed + jnp.dot(kl_ref[...], rhs, preferred_element_type=F32)
        for t in range(2):
            for g in range(group):
                image[(at + t) * group + g] = mixed[
                    g * size_x : (g + 1) * size_x, t * lanes : (t + 1) * lanes
                ]
        return carry

    lax.fori_loop(0, count // 2, one, 0)


def split_offset(offset):
    bits_y, bits_z = BOXY.bit_length() - 1, BOXZ.bit_length() - 1
    return offset >> (bits_y + bits_z), (offset >> bits_z) & (BOXY - 1), offset & (BOXZ - 1)


def pick_values(image, half, corner, offset):
    half_z, _, size_y = image.shape
    cols = offset.shape[-1]
    box_rows = BOXZ * BOXX
    at_x, at_y, at_z = corner & 255, (corner >> 8) & 255, corner >> 16
    from_z = at_z - half * half_z
    first = jnp.clip(from_z, 0, half_z - BOXZ)
    off_x, off_y, off_z = split_offset(offset)
    y_cell = at_y + off_y
    box_row = (off_z + (from_z - first)) * BOXX + off_x
    box = image[pl.ds(first, BOXZ), pl.ds(at_x, BOXX), :]
    box = box.reshape(box_rows, size_y).astype(BF16)
    y_line = lax.broadcasted_iota(jnp.int32, (size_y, cols), 0)
    pick_y = jnp.where(y_line == y_cell, 1.0, 0.0).astype(BF16)
    lines = jnp.dot(box, pick_y, preferred_element_type=F32)
    row_line = lax.broadcasted_iota(jnp.int32, (box_rows, cols), 0)
    line = jnp.where(row_line == box_row, lines, 0.0)
    return jnp.sum(line, axis=0, keepdims=True)


def pick_blocks(image, half, corner_ref, line, offsets_ref, base, values, first, count):
    unroll = min(16, count)

    def some(part, carry):
        for k in range(unroll):
            block = first + part * unroll + k
            values[pl.ds(block, 1), :] = pick_values(
                image, half, corner_ref[line, block], offsets_ref[pl.ds(base + block, 1), :]
            )
        return carry

    lax.fori_loop(0, count // unroll, some, 0)


def power_below(value):
    return 1 << (value.bit_length() - 1)


def two_parts(value):
    high = value.astype(BF16)
    return high, (value - high.astype(F32)).astype(BF16)


def dot_parts(left, right):
    (left_high, left_low), (right_high, right_low) = left, right
    small = lax.dot_general(left_high, right_low, NT, preferred_element_type=F32)
    small = small + lax.dot_general(left_low, right_high, NT, preferred_element_type=F32)
    return small + lax.dot_general(left_high, right_high, NT, preferred_element_type=F32)


def mix_planes(field_of, kern_y, kern_z, rows, planes_ref, slab):
    size_z = kern_z[0].shape[0]
    for x in range(slab):
        inner = dot_parts(kern_z, two_parts(field_of(x)))
        rows[pl.ds(x, size_z, stride=slab), :] = dot_parts(two_parts(inner), kern_y)
    planes_ref[...] = rows[...].astype(BF16).reshape(planes_ref.shape)


def planes_kernel(
    weights_ref,
    direction_ref,
    kern_x_ref,
    kern_y_ref,
    kern_z_ref,
    corner_ref,
    offsets_ref,
    out_u,
    out_d,
    kh_ref,
    kl_ref,
    packed_ref,
    offs_ref,
    rows,
    rows_d,
):
    slab = weights_ref.shape[0]
    kern_y, kern_z = two_parts(kern_y_ref[...]), two_parts(kern_z_ref[...])
    mix_planes(lambda x: weights_ref[x], kern_y, kern_z, rows, out_u, slab)
    mix_planes(lambda x: direction_ref[x], kern_y, kern_z, rows_d, out_d, slab)
    packed = corner_ref[0:1] + corner_ref[1:2] * 256 + corner_ref[2:3] * 65536
    packed_ref[...] = jnp.broadcast_to(packed, packed_ref.shape)
    offs_ref[...] = offsets_ref[...].astype(jnp.int16)
    size_x, wide = kern_x_ref.shape[0], kh_ref.shape[1]
    group = kh_ref.shape[0] // size_x
    pack = group * slab
    source = lax.broadcasted_iota(jnp.int32, (size_x, wide), 0)
    column = lax.broadcasted_iota(jnp.int32, (size_x, wide), 1)
    same = source == lax.div(column, pack) * slab + lax.rem(column, slab)
    layer = lax.div(lax.rem(column, pack), slab)
    for part, out_ref in zip(two_parts(kern_x_ref[...]), (kh_ref, kl_ref)):
        for g in range(group):
            select = jnp.where(same & (layer == g), 1.0, 0.0).astype(BF16)
            spot = jnp.dot(part, select, preferred_element_type=F32)
            out_ref[g * size_x : (g + 1) * size_x] = spot.astype(BF16)


def rank_blocks(corners, me, slab, ranks_ref, list_ref):
    devices, blocks = corners.shape
    from_x = (corners & 255) - me * slab
    touch = jnp.where((from_x < slab) & (from_x > -BOXX), 1.0, 0.0)
    earlier = lax.broadcasted_iota(jnp.int32, (blocks, blocks), 0)
    earlier = earlier < lax.broadcasted_iota(jnp.int32, (blocks, blocks), 1)
    within = jnp.dot(
        touch.astype(BF16), jnp.where(earlier, 1.0, 0.0).astype(BF16), preferred_element_type=F32
    )
    count = jnp.sum(touch, axis=1, keepdims=True)
    below = lax.broadcasted_iota(jnp.int32, (devices, devices), 1)
    below = below < lax.broadcasted_iota(jnp.int32, (devices, devices), 0)
    base = jnp.dot(
        jnp.where(below, 1.0, 0.0).astype(BF16),
        jnp.broadcast_to(count, (devices, blocks)).astype(BF16),
        preferred_element_type=F32,
    )
    ranks = jnp.where(touch > 0.0, base + within, -1.0)
    for device in range(devices):
        line = jnp.broadcast_to(ranks[device : device + 1], (blocks, blocks))
        ranks_ref[device] = jnp.transpose(line)
    total = jnp.sum(touch)
    list_ref[pl.ds(devices, 8), :] = jnp.full((8, blocks), total, F32).astype(jnp.int32)


def list_blocks(ranks_ref, list_ref, line):
    devices, blocks, _ = ranks_ref.shape
    wanted = lax.broadcasted_iota(jnp.int32, (blocks, blocks), 1) + line * blocks
    wanted = wanted.astype(F32)
    block = lax.broadcasted_iota(jnp.int32, (blocks, blocks), 0).astype(F32)

    def one(device, ids):
        hit = ranks_ref[device] == wanted
        start = (device * blocks).astype(F32)
        return ids + jnp.where(hit, block + start, 0.0)

    ids = lax.fori_loop(0, devices, one, jnp.zeros((blocks, blocks), F32))
    ids = jnp.sum(ids, axis=0, keepdims=True)
    list_ref[pl.ds(line, 1), :] = ids.astype(jnp.int32)


def log_sigmoid(value):
    return jnp.minimum(value, 0.0) - jnp.log1p(jnp.exp(-jnp.abs(value)))


def apply_interp(values, interp, outs, first, count):
    unroll = min(16, count)
    cols = values[0].shape[1]

    def some(part, carry):
        for k in range(unroll):
            block = first + part * unroll + k
            top = lax.broadcasted_iota(jnp.int32, (8, cols), 0)
            rows = jnp.broadcast_to(values[0][pl.ds(block, 1), :], (8, cols))
            for f in range(1, len(values)):
                rows = jnp.where(top == f, values[f][pl.ds(block, 1), :], rows)
            line = lax.dot_general(
                rows.astype(BF16), interp[block], NT, preferred_element_type=F32
            )
            for f, out_ref in enumerate(outs):
                out_ref[pl.ds(block, 1), :] = line[f : f + 1]
        return carry

    lax.fori_loop(0, count // unroll, some, 0)


def forward_kernel(
    group,
    trial_ref,
    accept_ref,
    own_u,
    own_d,
    packed_ref,
    offs_ref,
    kh_ref,
    kl_ref,
    offsets_ref,
    labels_ref,
    weights_ref,
    direction_ref,
    interp_ref,
    prob_ref,
    split_ref,
    list_ref,
    corners_ref,
    pair_packed,
    pair_offsets,
    all_offs,
    all_terms,
    buf_u,
    buf_d,
    all_packed,
    image_u,
    image_d,
    interp,
    mine_u,
    mine_d,
    theirs,
    out_u,
    out_d,
    in_u,
    in_d,
    mate_offs,
    mate_u,
    mate_d,
    latent_ref,
    slope_ref,
    res_ref,
    own_terms,
    weights_t,
    direction_t,
    ranks_ref,
    corner_smem,
    local_sem,
    mate_send,
    mate_recv,
    *sems,
):
    devices = buf_u.shape[0]
    blocks, per_block = labels_ref.shape
    slab, size_y, size_z = weights_ref.shape
    half_z, size_x, _ = image_u.shape
    place = Place(devices)
    load = pltpu.make_async_copy(interp_ref, interp, local_sem.at[0])
    load.start()
    u = Relay(place, own_u, buf_u, sems[0:4], halved=True)
    d = Relay(place, own_d, buf_d, sems[4:8], halved=True)
    o = Relay(place, offs_ref, all_offs, sems[8:12])
    t = Relay(place, own_terms, all_terms, sems[12:16])
    c = Relay(place, packed_ref, all_packed, sems[16:20])

    def swap(source, landing, k):
        return place.push(source, landing, mate_send.at[k], mate_recv.at[k], place.mate)

    mate_rows = pl.ds(pl.multiple_of(place.mate * slab, slab), slab)
    swaps = [
        swap(offs_ref, mate_offs, 0),
        swap(out_u, in_u, 1),
        swap(out_d, in_d, 2),
        swap(image_u.at[:, mate_rows, :], mate_u, 3),
        swap(image_d.at[:, mate_rows, :], mate_d, 4),
    ]
    place.greet()
    c.start_own()
    u.start_own()
    swaps[0].start()
    for relay in (c, u, d, o):
        relay.keep_own()
    pair_offsets[pl.ds(0, blocks)] = offsets_ref[...]
    for x in range(slab):
        weights_t[pl.ds(x, size_z, stride=slab), :] = jnp.transpose(weights_ref[x])
        direction_t[pl.ds(x, size_z, stride=slab), :] = jnp.transpose(direction_ref[x])

    def mixer(relay, image):
        return lambda piece: mix_depth(
            relay.buf, kh_ref, kl_ref, image, group, size_x, piece * relay.size, relay.size
        )

    u.run(mix=mixer(u, image_u), tail=d.start_own, riders=(c,))
    swaps[0].wait()
    pair_offsets[pl.ds(blocks, blocks)] = mate_offs[...].astype(jnp.int32)
    corners = all_packed[:, 0, :]
    corners_ref[...] = corners
    pair_packed[...] = jnp.concatenate([packed_ref[0:4], all_packed[place.mate, 0:4]], axis=0)
    rank_blocks(corners, place.me, slab, ranks_ref, list_ref)
    to_smem = pltpu.make_async_copy(pair_packed, corner_smem, local_sem.at[1])
    to_smem.start()
    to_smem.wait()
    steps = power_below(u.pieces + 2)
    some, lines = blocks // steps, -(-devices // steps)

    def pick(image, mine, first, count):
        line, base = (0, 0) if mine is not theirs else (4, blocks)
        pick_blocks(
            image, place.half, corner_smem, line, pair_offsets, base, mine, first, count
        )

    def early(step):
        pick(image_u, theirs, step * some, some)
        pick(image_u, mine_u, step * some, some)
        for k in range(lines):
            list_blocks(ranks_ref, list_ref, step * lines + k)

    d.run(work=early, steps=steps, mix=mixer(d, image_d), tail=o.start_own)
    swaps[3].start()
    out_u[...] = theirs[...].astype(BF16)
    pick(image_d, theirs, 0, blocks)
    swaps[1].start()
    out_d[...] = theirs[...].astype(BF16)
    o.line_events(0)
    pick(image_d, mine_d, 0, blocks // 4)
    swaps[2].start()
    pick(image_d, mine_d, blocks // 4, blocks - blocks // 4)
    swaps[4].start()
    o.side_events(0)
    swaps[1].wait()
    swaps[2].wait()
    mine_u[...] = mine_u[...] + in_u[...].astype(F32)
    mine_d[...] = mine_d[...] + in_d[...].astype(F32)
    load.wait()
    apply_interp((mine_u, mine_d), interp, (latent_ref, slope_ref), 0, blocks)
    slope = slope_ref[...]
    latent = latent_ref[...]
    prob = jax.nn.sigmoid(latent + trial_ref[accept_ref[0]] * slope)
    prob_ref[...] = prob
    target = labels_ref[...].astype(F32)
    res_ref[...] = (target - prob).astype(BF16).astype(F32)
    unroll = 16

    def back(step, carry):
        for k in range(unroll):
            block = step * unroll + k
            row = jnp.broadcast_to(res_ref[pl.ds(block, 1), :], (8, per_block))
            term = jnp.dot(row.astype(BF16), interp[block], preferred_element_type=F32)
            theirs[pl.ds(block, 1), :] = term[0:1]
        return carry

    lax.fori_loop(0, blocks // unroll, back, 0)
    own_terms[...] = theirs[...].astype(BF16)
    t.keep_own()
    o.twin_events(0)
    for relay in (c, u, d, o):
        relay.finish()
    t.start_own()
    swaps[3].wait()
    swaps[4].wait()
    own_rows = pl.ds(pl.multiple_of(place.me * slab, slab), slab)
    here_z = pl.ds(pl.multiple_of(place.half * half_z * slab, slab), half_z * slab)
    there_z = pl.ds(pl.multiple_of((1 - place.half) * half_z * slab, slab), half_z * slab)

    def quad(field_t, image, mate):
        both = (half_z * slab, size_y)
        near = field_t[here_z] * image[:, own_rows, :].reshape(both)
        return jnp.sum(near + field_t[there_z] * mate[...].reshape(both))

    signed = 2.0 * target - 1.0
    line = lax.broadcasted_iota(jnp.int32, (8, 128), 0)
    lane = lax.broadcasted_iota(jnp.int32, (8, 128), 1)
    sums = jnp.zeros((8, 128), F32)
    for k in range(NTRIAL):
        at_trial = latent + trial_ref[k] * slope
        loglik = jnp.sum(log_sigmoid(signed * at_trial))
        descent = jnp.sum((target - jax.nn.sigmoid(at_trial)) * slope)
        sums = jnp.where((line == 0) & (lane == k), loglik, sums)
        sums = jnp.where((line == 1) & (lane == k), descent, sums)
    sums = jnp.where(line == 2, quad(weights_t, image_u, mate_u), sums)
    sums = jnp.where(line == 3, quad(direction_t, image_u, mate_u), sums)
    sums = jnp.where(line == 4, quad(direction_t, image_d, mate_d), sums)
    first = sums.astype(BF16).astype(F32)
    second = (sums - first).astype(BF16).astype(F32)
    third = sums - first - second
    split_ref[...] = jnp.concatenate([first, second, third], axis=0).astype(BF16)
    t.run()
    t.finish()


def bend_kernel(
    group,
    points,
    corner_smem,
    trial_ref,
    own_ref,
    split_ref,
    kh_ref,
    kl_ref,
    pair_offsets,
    prob_ref,
    interp_ref,
    out_ref,
    trials_ref,
    buf,
    all_split,
    image,
    interp,
    mine,
    theirs,
    sent,
    got,
    local_sem,
    mate_send,
    mate_recv,
    *sems,
):
    devices = buf.shape[0]
    blocks = prob_ref.shape[0]
    size_x = image.shape[1]
    place = Place(devices)
    load = pltpu.make_async_copy(interp_ref, interp, local_sem)
    load.start()
    b = Relay(place, own_ref, buf, sems[0:4], halved=True)
    s = Relay(place, split_ref, all_split, sems[4:8])
    swap = place.push(sent, got, mate_send, mate_recv, place.mate)
    place.greet()
    s.start_own()
    b.start_own()
    b.keep_own()
    s.keep_own()
    b.run(
        mix=lambda piece: mix_depth(
            buf, kh_ref, kl_ref, image, group, size_x, piece * b.size, b.size
        ),
        riders=(s,),
    )

    def pick(line, base, values, first, count):
        pick_blocks(
            image, place.half, corner_smem, line, pair_offsets, base, values, first, count
        )

    pick(4, blocks, theirs, 0, blocks)
    sent[...] = theirs[...].astype(BF16)
    pick(0, 0, mine, 0, blocks // 4)
    swap.start()
    pick(0, 0, mine, blocks // 4, blocks - blocks // 4)
    total = jnp.sum(all_split[...].astype(F32), axis=0)
    total = total[0:8] + total[8:16] + total[16:24]
    lane = lax.broadcasted_iota(jnp.int32, (1, 128), 1)
    step = jnp.zeros((1, 128), F32)
    for k in range(NTRIAL):
        step = jnp.where(lane == k, trial_ref[k], step)
    loglik, descent, quad_gu, quad_du, quad_dv = (total[k : k + 1] for k in range(5))
    prior = 0.5 * (quad_gu + 2.0 * step * quad_du + step * step * quad_dv)
    trials_ref[0:1] = (loglik - prior) / points
    trials_ref[1:2] = (descent - quad_du - step * quad_dv) / points
    load.wait()
    swap.wait()
    mine[...] = mine[...] + got[...].astype(F32)
    apply_interp((mine,), interp, (out_ref,), 0, blocks)
    prob = prob_ref[...]
    out_ref[...] = prob * (1.0 - prob) * out_ref[...]
    b.finish()
    s.finish()


def spread_kernel(
    list_ref,
    corners_ref,
    trial_ref,
    accept_ref,
    offs_ref,
    terms_ref,
    weights_ref,
    direction_ref,
    kern_y_ref,
    kern_z_ref,
    new_ref,
    grad_ref,
    planes_ref,
    offs,
    terms,
    spread,
):
    devices, blocks, cols = offs_ref.shape
    slab, size_y, size_z = weights_ref.shape
    rows = BOXZ * slab
    unroll = 8
    me = lax.axis_index("pts")
    spread[...] = jnp.zeros_like(spread)

    def widen(device, carry):
        offs[pl.ds(pl.multiple_of(device * blocks, blocks), blocks)] = offs_ref[device].astype(
            jnp.int32
        )
        terms[pl.ds(pl.multiple_of(device * blocks, blocks), blocks)] = terms_ref[device].astype(
            F32
        )
        return carry

    lax.fori_loop(0, devices, widen, 0)
    count = list_ref[devices, 0]

    def some(part, carry):
        sums = []
        for k in range(unroll):
            at = part * unroll + k
            block = list_ref[lax.div(at, blocks), lax.rem(at, blocks)]
            packed = corners_ref[lax.div(block, blocks), lax.rem(block, blocks)]
            from_x = jnp.where(at < count, (packed & 255) - me * slab, -2 * BOXX)
            at_y = (packed >> 8) & 255
            at_z = packed >> 16
            off_x, off_y, off_z = split_offset(offs[pl.ds(block, 1), :])
            cell = off_x + from_x
            key = jnp.where((cell >= 0) & (cell < slab), off_z * slab + cell, -1)
            y_cell = off_y + at_y
            row_line = lax.broadcasted_iota(jnp.int32, (rows, cols), 0)
            y_line = lax.broadcasted_iota(jnp.int32, (size_y, cols), 0)
            left = jnp.where(row_line == key, terms[pl.ds(block, 1), :], 0.0).astype(BF16)
            right = jnp.where(y_line == y_cell, 1.0, 0.0).astype(BF16)
            sums.append((at_z, lax.dot_general(left, right, NT, preferred_element_type=F32)))
        for at_z, piece in sums:
            spread[pl.ds(pl.multiple_of(at_z * slab, slab), rows), :] += piece
        return carry

    lax.fori_loop(0, lax.div(count + unroll - 1, unroll), some, 0)
    chosen = trial_ref[accept_ref[0]]
    for x in range(slab):
        new = weights_ref[x] + chosen * direction_ref[x]
        new_ref[x] = new
        grad_ref[x] = jnp.transpose(spread[pl.ds(x, size_z, stride=slab), :]) - new
    kern_y, kern_z = two_parts(kern_y_ref[...]), two_parts(kern_z_ref[...])
    mix_planes(lambda x: grad_ref[x], kern_y, kern_z, spread, planes_ref, slab)


def body(
    grid_weights,
    direction,
    kern_x,
    kern_y,
    kern_z,
    interp,
    block_corner,
    block_offsets,
    labels,
    trial_steps,
    accept,
):
    slab, size_y, size_z = grid_weights.shape
    size_x = kern_x.shape[0]
    devices = lax.axis_size("pts")
    blocks, cols = block_offsets.shape
    per_block = interp.shape[1]
    points = blocks * per_block * devices
    group = max(1, PACK // slab)
    pack = group * slab
    units = size_z // group
    pieces = max(1, 64 // devices)

    smem = pl.BlockSpec(memory_space=pltpu.SMEM)
    vmem = pl.BlockSpec(memory_space=pltpu.VMEM)
    hbm = pl.BlockSpec(memory_space=pl.ANY)
    limit = dict(vmem_limit_bytes=VMEM_BYTES)
    planes_shape = jax.ShapeDtypeStruct((units, pack, size_y), BF16)
    rows_scratch = pltpu.VMEM((size_z * slab, size_y), F32)
    planes_scratch = pltpu.VMEM((devices, units // 2, pack, size_y), BF16)
    image_scratch = pltpu.VMEM((size_z // 2, size_x, size_y), F32)
    interp_scratch = pltpu.VMEM(interp.shape, BF16)
    point_scratch = pltpu.VMEM((blocks, per_block), F32)
    point_shape = jax.ShapeDtypeStruct((blocks, per_block), F32)

    wide_shape = jax.ShapeDtypeStruct((group * size_x, devices * pack), BF16)
    planes_w, planes_d, kern_high, kern_low, packed, offs = pl.pallas_call(
        planes_kernel,
        in_specs=[vmem] * 7,
        out_specs=[vmem] * 6,
        out_shape=[
            planes_shape,
            planes_shape,
            wide_shape,
            wide_shape,
            jax.ShapeDtypeStruct((8, blocks), jnp.int32),
            jax.ShapeDtypeStruct((blocks, cols), jnp.int16),
        ],
        scratch_shapes=[rows_scratch, rows_scratch],
        compiler_params=pltpu.CompilerParams(**limit),
        name="planes",
    )(grid_weights, direction, kern_x, kern_y, kern_z, block_corner, block_offsets)

    pick_scratch = pltpu.VMEM((blocks, cols), F32)
    swap_scratch = pltpu.VMEM((blocks, cols), BF16)
    mate_scratch = pltpu.VMEM((size_z // 2, slab, size_y), F32)
    probability, split, block_list, corners, pair_packed, pair_offsets, offsets, terms = (
        pl.pallas_call(
            functools.partial(forward_kernel, group),
            in_specs=[smem] * 2 + [vmem] * 10 + [hbm],
            out_specs=[vmem] * 8,
            out_shape=[
                point_shape,
                jax.ShapeDtypeStruct((24, 128), BF16),
                jax.ShapeDtypeStruct((devices + 8, blocks), jnp.int32),
                jax.ShapeDtypeStruct((devices, blocks), jnp.int32),
                jax.ShapeDtypeStruct((8, blocks), jnp.int32),
                jax.ShapeDtypeStruct((2 * blocks, cols), jnp.int32),
                jax.ShapeDtypeStruct((devices, blocks, cols), jnp.int16),
                jax.ShapeDtypeStruct((devices, blocks, cols), BF16),
            ],
            scratch_shapes=[
                planes_scratch,
                planes_scratch,
                pltpu.VMEM((devices, 8, blocks), jnp.int32),
                image_scratch,
                image_scratch,
                interp_scratch,
                pick_scratch,
                pick_scratch,
                pick_scratch,
                swap_scratch,
                swap_scratch,
                swap_scratch,
                swap_scratch,
                pltpu.VMEM((blocks, cols), jnp.int16),
                mate_scratch,
                mate_scratch,
                point_scratch,
                point_scratch,
                point_scratch,
                swap_scratch,
                rows_scratch,
                rows_scratch,
                pltpu.VMEM((devices, blocks, blocks), F32),
                pltpu.SMEM((8, blocks), jnp.int32),
                pltpu.SemaphoreType.DMA((2,)),
                pltpu.SemaphoreType.DMA((5,)),
                pltpu.SemaphoreType.DMA((5,)),
                *relay_sems(devices, pieces),
                *relay_sems(devices, pieces),
                *relay_sems(devices, 1),
                *relay_sems(devices, 1),
                *relay_sems(devices, 1),
            ],
            compiler_params=pltpu.CompilerParams(
                collective_id=0, has_side_effects=True, **limit
            ),
            name="forward",
        )(
            trial_steps,
            accept,
            planes_w,
            planes_d,
            packed,
            offs,
            kern_high,
            kern_low,
            block_offsets,
            labels,
            grid_weights,
            direction,
            interp,
        )
    )

    new_weights, grid_gradient, bend_planes = pl.pallas_call(
        spread_kernel,
        in_specs=[smem] * 4 + [vmem] * 6,
        out_specs=[vmem] * 3,
        out_shape=[
            jax.ShapeDtypeStruct(grid_weights.shape, F32),
            jax.ShapeDtypeStruct(grid_weights.shape, F32),
            planes_shape,
        ],
        scratch_shapes=[
            pltpu.VMEM((devices * blocks, cols), jnp.int32),
            pltpu.VMEM((devices * blocks, cols), F32),
            rows_scratch,
        ],
        compiler_params=pltpu.CompilerParams(**limit),
        name="spread",
    )(
        block_list,
        corners,
        trial_steps,
        accept,
        offsets,
        terms,
        grid_weights,
        direction,
        kern_y,
        kern_z,
    )

    curvature, trials = pl.pallas_call(
        functools.partial(bend_kernel, group, points),
        in_specs=[smem] * 2 + [vmem] * 6 + [hbm],
        out_specs=[vmem] * 2,
        out_shape=[point_shape, jax.ShapeDtypeStruct((2, 128), F32)],
        scratch_shapes=[
            planes_scratch,
            pltpu.VMEM((devices, 24, 128), BF16),
            image_scratch,
            interp_scratch,
            pick_scratch,
            pick_scratch,
            swap_scratch,
            swap_scratch,
            pltpu.SemaphoreType.DMA,
            pltpu.SemaphoreType.DMA,
            pltpu.SemaphoreType.DMA,
            *relay_sems(devices, pieces),
            *relay_sems(devices, 1),
        ],
        compiler_params=pltpu.CompilerParams(collective_id=1, has_side_effects=True, **limit),
        name="bend",
    )(
        pair_packed,
        trial_steps,
        bend_planes,
        split,
        kern_high,
        kern_low,
        pair_offsets,
        probability,
        interp,
    )
    return (new_weights, grid_gradient, curvature, trials[0, :NTRIAL], trials[1, :NTRIAL])


def solution(mesh):
    return jax.shard_map(
        body,
        mesh=mesh,
        in_specs=(
            P(("parts", "pts"), None, None),
            P(("parts", "pts"), None, None),
            P(),
            P(),
            P(),
            P(("parts", "pts"), None, None),
            P(None, ("parts", "pts")),
            P(("parts", "pts"), None),
            P(("parts", "pts"), None),
            P(),
            P(),
        ),
        out_specs=(
            P(("parts", "pts"), None, None),
            P(("parts", "pts"), None, None),
            P(("parts", "pts"), None),
            P("parts"),
            P("parts"),
        ),
        check_vma=False,
    )
```

time: 191 us -> 151 us (0.79)
  Pallas kernels: 179 us -> 147 us
  other arithmetic: 4.92 us -> 0 us
    pallas_call x1, Pallas kernels: 108 us -> 82.5 us  [body(): pl.pallas_call(functools.partial(forward_kernel, group), in_specs=[smem]...]
    pallas_call x2, Pallas kernels: 60.3 us -> 53.8 us  [the longest x1 49.7 us: body(): pl.pallas_call(functools.partial(bend_kernel, group, points), in_specs=[s...]
    div x1 -> x0, other arithmetic: 3.2 us -> none  [body(): trial_slope = (descent - quad_du - trial_steps * quad_dv) / points]
where the time goes in v2:
time: 151 us
  Pallas kernels  147 us (97%)
  local copies, waits for them, and re-layouts  2.7 us (2%)
    pallas_call x1, Pallas kernels, body(): pl.pallas_call(functools.partial(forward_kernel, group), in_specs=[smem]...  82.5 us
    pallas_call x1, Pallas kernels, body(): pl.pallas_call(functools.partial(bend_kernel, group, points), in_specs=[s...  49.7 us
    pallas_call x1, Pallas kernels, body(): pl.pallas_call(spread_kernel, in_specs=[smem] * 4 + [vmem] * 6, out_specs...  10.5 us
    pallas_call x1, Pallas kernels, body(): pl.pallas_call(planes_kernel, in_specs=[vmem] * 7, out_specs=[vmem] * 6,...  4.12 us

profile of v2, /device:TPU:0, one launch (start us, length us, event | category | flops | bytes accessed | tf_op | source)
XLA Modules:
  0.0 150.8 jit_solution(17910372127976837708)
XLA Ops:
  1.3 4.1 %planes.1 = (bf16[64,16,128]{2,1,0:T(8,128)(2,1)}, bf16[64,16,128]{2,1,0:T(8,128)(2,1)}, bf16[256,256]{1,0:T(8,128)(2,1)}, bf16[256,256]{1,0:T(8,128)(2,1)}, s32[8,128]{1,0:T(8,128)}, /*index=5*/s16[128,256]{1,0:T(8,128)(2,1)}) custom-call(f32[8,128,128]{2,1,0:T(8,128)} %weights_ref.5, f32[8,128,128]{2,1,0:T(8,128)} %direction_ref.5, f32[128,128]{1,0:T(8,128)} %kern_x_ref.1, ...), custom_call_target="tpu_custom_call" | custom-call | tf_op jit(solution)/shard_map/planes/pallas_call | solution.py:823
  5.4 82.5 %forward.1 = (f32[128,128]{1,0:T(8,128)}, bf16[24,128]{1,0:T(8,128)(2,1)}, s32[24,128]{1,0:T(8,128)}, s32[16,128]{1,0:T(8,128)}, s32[8,128]{1,0:T(8,128)}, /*ind...) custom-call(f32[5]{0:T(128)} %trial_ref.5, s32[1]{0:T(128)S(6)} %copy.17.accept_ref, ...), custom_call_target="tpu_custom_call" | custom-call | tf_op jit(solution)/shard_map/forward/pallas_call | solution.py:844
  87.9 10.5 %spread.1 = (f32[8,128,128]{2,1,0:T(8,128)}, f32[8,128,128]{2,1,0:T(8,128)}, bf16[64,16,128]{2,1,0:T(8,128)(2,1)}) custom-call(s32[24,128]{1,0:T(8,128)} %get-tuple-element.30.list_ref, s32[16,128]{1,0:T(8,128)} %get-tuple-element.31.corners_ref, f32[5]{0:T(128)} %trial_ref.5, s32[1]{0:T(128)S(6)} %copy.17.accept_ref, ...), custom_call_target="tpu_custom_call" | custom-call | tf_op jit(solution)/shard_map/spread/pallas_call | solution.py:913
  98.4 49.7 %bend.1 = (f32[128,128]{1,0:T(8,128)}, f32[2,128]{1,0:T(2,128)}) custom-call(s32[8,128]{1,0:T(8,128)} %get-tuple-element.36.corner_smem, f32[5]{0:T(128)} %trial_ref.5, bf16[64,16,128]{2,1,0:T(8,128)(2,1)} %get-tuple-element.37.own_ref, bf16[24,128]{1,0:T(8,128)(2,1)} %get-tuple-element.38.split_ref, bf16[256,256]{1,0:T(8,128)(2,1)} %get-tuple-element.28.kh_ref, ...), custom_call_target="tpu_custom_call" | custom-call | tf_op jit(solution)/shard_map/bend/pallas_call | solution.py:942
  148.1 1.2 slice_bitcast_fusion
  149.3 1.5 copy.18

commit v3 on v2

--- a/solution.py
+++ b/solution.py
@@ -12,6 +12,8 @@
 BOXZ = 8
 NTRIAL = 5
 PACK = 16
+BESIDE = 4
+UNROLL = 32
 VMEM_BYTES = 62 * 1024 * 1024
 
 F32 = jnp.float32
@@ -64,7 +66,9 @@
         self.others(lambda depth: tell(self.along(depth)))
         tell(self.beside)
         tell(self.twin)
-        pl.semaphore_wait(barrier, self.depths + 1)
+
+    def meet(self):
+        pl.semaphore_wait(pltpu.get_barrier_semaphore(), self.depths + 1)
 
     def push(self, source, landing, send_sem, recv_sem, device):
         return pltpu.make_async_remote_copy(
@@ -143,13 +147,15 @@
         first = here.half * count if self.halved else 0
         self.buf[here.me] = self.own[pl.ds(first, count)]
 
+    def start_piece(self, piece):
+        here = self.place
+        here.others(lambda depth: self.line_copy(piece, depth).start())
+        self.side_copy(piece, here.depth, mine=True).start()
+        self.twin_copy(piece, here.depth, here.side, mine=True).start()
+
     def start_own(self):
-        here = self.place
-
         def one(piece, carry):
-            here.others(lambda depth: self.line_copy(piece, depth).start())
-            self.side_copy(piece, here.depth, mine=True).start()
-            self.twin_copy(piece, here.depth, here.side, mine=True).start()
+            self.start_piece(piece)
             return carry
 
         lax.fori_loop(0, self.pieces, one, 0)
@@ -287,25 +293,36 @@
 def pick_values(image, half, corner, offset):
     half_z, _, size_y = image.shape
     cols = offset.shape[-1]
-    box_rows = BOXZ * BOXX
     at_x, at_y, at_z = corner & 255, (corner >> 8) & 255, corner >> 16
     from_z = at_z - half * half_z
     first = jnp.clip(from_z, 0, half_z - BOXZ)
     off_x, off_y, off_z = split_offset(offset)
-    y_cell = at_y + off_y
-    box_row = (off_z + (from_z - first)) * BOXX + off_x
+    cell_z = off_z + (from_z - first)
+    wide = BESIDE * BOXY
+    box_rows = BOXZ // BESIDE * BOXX
+    box_row = (cell_z >> (BESIDE.bit_length() - 1)) * BOXX + off_x
+    box_cell = (cell_z & (BESIDE - 1)) * BOXY + off_y
     box = image[pl.ds(first, BOXZ), pl.ds(at_x, BOXX), :]
-    box = box.reshape(box_rows, size_y).astype(BF16)
-    y_line = lax.broadcasted_iota(jnp.int32, (size_y, cols), 0)
-    pick_y = jnp.where(y_line == y_cell, 1.0, 0.0).astype(BF16)
-    lines = jnp.dot(box, pick_y, preferred_element_type=F32)
+    lane = lax.broadcasted_iota(jnp.int32, (BOXX, size_y), 1)
+    groups = []
+    for z in range(0, BOXZ, BESIDE):
+        group = pltpu.roll(box[z], lax.rem(size_y - at_y, size_y), axis=1)
+        for k in range(1, BESIDE):
+            shift = lax.rem(size_y + k * BOXY - at_y, size_y)
+            plane = pltpu.roll(box[z + k], shift, axis=1)
+            group = jnp.where(lane >= k * BOXY, plane, group)
+        groups.append(group[:, :wide])
+    box = jnp.concatenate(groups, axis=0).astype(BF16)
+    cell_line = lax.broadcasted_iota(jnp.int32, (wide, cols), 0)
+    pick_cell = jnp.where(cell_line == box_cell, 1.0, 0.0).astype(BF16)
+    lines = jnp.dot(box, pick_cell, preferred_element_type=F32)
     row_line = lax.broadcasted_iota(jnp.int32, (box_rows, cols), 0)
     line = jnp.where(row_line == box_row, lines, 0.0)
     return jnp.sum(line, axis=0, keepdims=True)
 
 
 def pick_blocks(image, half, corner_ref, line, offsets_ref, base, values, first, count):
-    unroll = min(16, count)
+    unroll = min(UNROLL, count)
 
     def some(part, carry):
         for k in range(unroll):
@@ -426,7 +443,7 @@
 
 
 def apply_interp(values, interp, outs, first, count):
-    unroll = min(16, count)
+    unroll = min(UNROLL, count)
     cols = values[0].shape[1]
 
     def some(part, carry):
@@ -483,6 +500,8 @@
     in_u,
     in_d,
     mate_offs,
+    rows_u,
+    rows_d,
     mate_u,
     mate_d,
     latent_ref,
@@ -514,24 +533,24 @@
     def swap(source, landing, k):
         return place.push(source, landing, mate_send.at[k], mate_recv.at[k], place.mate)
 
-    mate_rows = pl.ds(pl.multiple_of(place.mate * slab, slab), slab)
     swaps = [
         swap(offs_ref, mate_offs, 0),
         swap(out_u, in_u, 1),
         swap(out_d, in_d, 2),
-        swap(image_u.at[:, mate_rows, :], mate_u, 3),
-        swap(image_d.at[:, mate_rows, :], mate_d, 4),
+        swap(rows_u, mate_u, 3),
+        swap(rows_d, mate_d, 4),
     ]
     place.greet()
-    c.start_own()
-    u.start_own()
-    swaps[0].start()
     for relay in (c, u, d, o):
         relay.keep_own()
     pair_offsets[pl.ds(0, blocks)] = offsets_ref[...]
     for x in range(slab):
         weights_t[pl.ds(x, size_z, stride=slab), :] = jnp.transpose(weights_ref[x])
         direction_t[pl.ds(x, size_z, stride=slab), :] = jnp.transpose(direction_ref[x])
+    place.meet()
+    c.start_own()
+    u.start_own()
+    swaps[0].start()
 
     def mixer(relay, image):
         return lambda piece: mix_depth(
@@ -557,53 +576,70 @@
             image, place.half, corner_smem, line, pair_offsets, base, mine, first, count
         )
 
+    both = (half_z * slab, size_y)
+    mate_rows = pl.ds(pl.multiple_of(place.mate * slab, slab), slab)
+
     def early(step):
         pick(image_u, theirs, step * some, some)
         pick(image_u, mine_u, step * some, some)
         for k in range(lines):
             list_blocks(ranks_ref, list_ref, step * lines + k)
 
-    d.run(work=early, steps=steps, mix=mixer(d, image_d), tail=o.start_own)
-    swaps[3].start()
-    out_u[...] = theirs[...].astype(BF16)
+        @pl.when(step == steps - 1)
+        def _():
+            out_u[...] = theirs[...].astype(BF16)
+            rows_u[...] = image_u[:, mate_rows, :].reshape(both).astype(BF16)
+
+    d.run(work=early, steps=steps, mix=mixer(d, image_d))
+    swaps[1].start()
     pick(image_d, theirs, 0, blocks)
-    swaps[1].start()
     out_d[...] = theirs[...].astype(BF16)
-    o.line_events(0)
+    rows_d[...] = image_d[:, mate_rows, :].reshape(both).astype(BF16)
     pick(image_d, mine_d, 0, blocks // 4)
     swaps[2].start()
+    o.start_own()
     pick(image_d, mine_d, blocks // 4, blocks - blocks // 4)
+    swaps[1].wait()
+    mine_u[...] = mine_u[...] + in_u[...].astype(F32)
+    load.wait()
+    swaps[2].wait()
+    swaps[3].start()
     swaps[4].start()
+    mine_d[...] = mine_d[...] + in_d[...].astype(F32)
+    target = labels_ref[...].astype(F32)
+    part = blocks // 2
+    unroll = min(UNROLL, part)
+
+    def back(first):
+        def one(step, carry):
+            for k in range(unroll):
+                block = first + step * unroll + k
+                row = jnp.broadcast_to(res_ref[pl.ds(block, 1), :], (8, per_block))
+                term = jnp.dot(row.astype(BF16), interp[block], preferred_element_type=F32)
+                theirs[pl.ds(block, 1), :] = term[0:1]
+            return carry
+
+        lax.fori_loop(0, part // unroll, one, 0)
+
+    for piece in range(2):
+        rows = slice(piece * part, (piece + 1) * part)
+        apply_interp((mine_u, mine_d), interp, (latent_ref, slope_ref), piece * part, part)
+        if piece > 0:
+            t.start_piece(0)
+            o.line_events(0)
+        prob = jax.nn.sigmoid(latent_ref[rows] + trial_ref[accept_ref[0]] * slope_ref[rows])
+        prob_ref[rows] = prob
+        res_ref[rows] = (target[rows] - prob).astype(BF16).astype(F32)
+        back(piece * part)
+        own_terms[rows] = theirs[rows].astype(BF16)
     o.side_events(0)
-    swaps[1].wait()
-    swaps[2].wait()
-    mine_u[...] = mine_u[...] + in_u[...].astype(F32)
-    mine_d[...] = mine_d[...] + in_d[...].astype(F32)
-    load.wait()
-    apply_interp((mine_u, mine_d), interp, (latent_ref, slope_ref), 0, blocks)
+    t.keep_own()
+    for relay in (c, u, d):
+        relay.finish()
+    t.start_piece(1)
+    t.line_events(0)
     slope = slope_ref[...]
     latent = latent_ref[...]
-    prob = jax.nn.sigmoid(latent + trial_ref[accept_ref[0]] * slope)
-    prob_ref[...] = prob
-    target = labels_ref[...].astype(F32)
-    res_ref[...] = (target - prob).astype(BF16).astype(F32)
-    unroll = 16
-
-    def back(step, carry):
-        for k in range(unroll):
-            block = step * unroll + k
-            row = jnp.broadcast_to(res_ref[pl.ds(block, 1), :], (8, per_block))
-            term = jnp.dot(row.astype(BF16), interp[block], preferred_element_type=F32)
-            theirs[pl.ds(block, 1), :] = term[0:1]
-        return carry
-
-    lax.fori_loop(0, blocks // unroll, back, 0)
-    own_terms[...] = theirs[...].astype(BF16)
-    t.keep_own()
-    o.twin_events(0)
-    for relay in (c, u, d, o):
-        relay.finish()
-    t.start_own()
     swaps[3].wait()
     swaps[4].wait()
     own_rows = pl.ds(pl.multiple_of(place.me * slab, slab), slab)
@@ -611,9 +647,8 @@
     there_z = pl.ds(pl.multiple_of((1 - place.half) * half_z * slab, slab), half_z * slab)
 
     def quad(field_t, image, mate):
-        both = (half_z * slab, size_y)
         near = field_t[here_z] * image[:, own_rows, :].reshape(both)
-        return jnp.sum(near + field_t[there_z] * mate[...].reshape(both))
+        return jnp.sum(near + field_t[there_z] * mate[...].astype(F32))
 
     signed = 2.0 * target - 1.0
     line = lax.broadcasted_iota(jnp.int32, (8, 128), 0)
@@ -632,7 +667,13 @@
     second = (sums - first).astype(BF16).astype(F32)
     third = sums - first - second
     split_ref[...] = jnp.concatenate([first, second, third], axis=0).astype(BF16)
-    t.run()
+    t.side_events(0)
+    t.line_events(1)
+    o.twin_events(0)
+    t.side_events(1)
+    t.twin_events(0)
+    o.finish()
+    t.twin_events(1)
     t.finish()
 
 
@@ -673,10 +714,11 @@
     s = Relay(place, split_ref, all_split, sems[4:8])
     swap = place.push(sent, got, mate_send, mate_recv, place.mate)
     place.greet()
+    b.keep_own()
+    s.keep_own()
+    place.meet()
     s.start_own()
     b.start_own()
-    b.keep_own()
-    s.keep_own()
     b.run(
         mix=lambda piece: mix_depth(
             buf, kh_ref, kl_ref, image, group, size_x, piece * b.size, b.size
@@ -735,7 +777,7 @@
     devices, blocks, cols = offs_ref.shape
     slab, size_y, size_z = weights_ref.shape
     rows = BOXZ * slab
-    unroll = 8
+    unroll = UNROLL
     me = lax.axis_index("pts")
     spread[...] = jnp.zeros_like(spread)
 
@@ -763,12 +805,13 @@
             off_x, off_y, off_z = split_offset(offs[pl.ds(block, 1), :])
             cell = off_x + from_x
             key = jnp.where((cell >= 0) & (cell < slab), off_z * slab + cell, -1)
-            y_cell = off_y + at_y
             row_line = lax.broadcasted_iota(jnp.int32, (rows, cols), 0)
-            y_line = lax.broadcasted_iota(jnp.int32, (size_y, cols), 0)
+            y_line = lax.broadcasted_iota(jnp.int32, (BOXY, cols), 0)
             left = jnp.where(row_line == key, terms[pl.ds(block, 1), :], 0.0).astype(BF16)
-            right = jnp.where(y_line == y_cell, 1.0, 0.0).astype(BF16)
-            sums.append((at_z, lax.dot_general(left, right, NT, preferred_element_type=F32)))
+            right = jnp.where(y_line == off_y, 1.0, 0.0).astype(BF16)
+            piece = lax.dot_general(left, right, NT, preferred_element_type=F32)
+            piece = jnp.concatenate([piece, jnp.zeros((rows, size_y - BOXY), F32)], axis=1)
+            sums.append((at_z, pltpu.roll(piece, at_y, axis=1)))
         for at_z, piece in sums:
             spread[pl.ds(pl.multiple_of(at_z * slab, slab), rows), :] += piece
         return carry
@@ -839,7 +882,7 @@
 
     pick_scratch = pltpu.VMEM((blocks, cols), F32)
     swap_scratch = pltpu.VMEM((blocks, cols), BF16)
-    mate_scratch = pltpu.VMEM((size_z // 2, slab, size_y), F32)
+    mate_scratch = pltpu.VMEM((size_z // 2 * slab, size_y), BF16)
     probability, split, block_list, corners, pair_packed, pair_offsets, offsets, terms = (
         pl.pallas_call(
             functools.partial(forward_kernel, group),
@@ -872,6 +915,8 @@
                 pltpu.VMEM((blocks, cols), jnp.int16),
                 mate_scratch,
                 mate_scratch,
+                mate_scratch,
+                mate_scratch,
                 point_scratch,
                 point_scratch,
                 point_scratch,
@@ -886,7 +931,7 @@
                 *relay_sems(devices, pieces),
                 *relay_sems(devices, pieces),
                 *relay_sems(devices, 1),
-                *relay_sems(devices, 1),
+                *relay_sems(devices, 2),
                 *relay_sems(devices, 1),
             ],
             compiler_params=pltpu.CompilerParams(

time: 151 us -> 135 us (0.89)
  Pallas kernels: 147 us -> 131 us
    pallas_call x1, Pallas kernels: 49.7 us -> 41.1 us  [body(): pl.pallas_call(functools.partial(bend_kernel, group, points), in_specs=[s...]
    pallas_call x1, Pallas kernels: 82.5 us -> 78.3 us  [body(): pl.pallas_call(functools.partial(forward_kernel, group), in_specs=[smem]...]
    pallas_call x1, Pallas kernels: 10.5 us -> 7.49 us  [body(): pl.pallas_call(spread_kernel, in_specs=[smem] * 4 + [vmem] * 6, out_specs...]
where the time goes in v3:
time: 135 us
  Pallas kernels  131 us (97%)
  local copies, waits for them, and re-layouts  2.7 us (2%)
    pallas_call x1, Pallas kernels, body(): pl.pallas_call(functools.partial(forward_kernel, group), in_specs=[smem]...  78.3 us
    pallas_call x1, Pallas kernels, body(): pl.pallas_call(functools.partial(bend_kernel, group, points), in_specs=[s...  41.1 us
    pallas_call x1, Pallas kernels, body(): pl.pallas_call(spread_kernel, in_specs=[smem] * 4 + [vmem] * 6, out_specs...  7.49 us
    pallas_call x1, Pallas kernels, body(): pl.pallas_call(planes_kernel, in_specs=[vmem] * 7, out_specs=[vmem] * 6,...  4.12 us

profile of v3, /device:TPU:0, one launch (start us, length us, event | category | flops | bytes accessed | tf_op | source)
XLA Modules:
  0.0 135.1 jit_solution(6330759835731743032)
XLA Ops:
  1.3 4.1 %planes.1 = (bf16[64,16,128]{2,1,0:T(8,128)(2,1)}, bf16[64,16,128]{2,1,0:T(8,128)(2,1)}, bf16[256,256]{1,0:T(8,128)(2,1)}, bf16[256,256]{1,0:T(8,128)(2,1)}, s32[8,128]{1,0:T(8,128)}, /*index=5*/s16[128,256]{1,0:T(8,128)(2,1)}) custom-call(f32[8,128,128]{2,1,0:T(8,128)} %weights_ref.5, f32[8,128,128]{2,1,0:T(8,128)} %direction_ref.5, f32[128,128]{1,0:T(8,128)} %kern_x_ref.1, ...), custom_call_target="tpu_custom_call" | custom-call | tf_op jit(solution)/shard_map/planes/pallas_call | solution.py:866
  5.4 78.3 %forward.1 = (f32[128,128]{1,0:T(8,128)}, bf16[24,128]{1,0:T(8,128)(2,1)}, s32[24,128]{1,0:T(8,128)}, s32[16,128]{1,0:T(8,128)}, s32[8,128]{1,0:T(8,128)}, /*ind...) custom-call(f32[5]{0:T(128)} %trial_ref.5, s32[1]{0:T(128)S(6)} %copy.17.accept_ref, ...), custom_call_target="tpu_custom_call" | custom-call | tf_op jit(solution)/shard_map/forward/pallas_call | solution.py:887
  83.7 7.5 %spread.1 = (f32[8,128,128]{2,1,0:T(8,128)}, f32[8,128,128]{2,1,0:T(8,128)}, bf16[64,16,128]{2,1,0:T(8,128)(2,1)}) custom-call(s32[24,128]{1,0:T(8,128)} %get-tuple-element.30.list_ref, s32[16,128]{1,0:T(8,128)} %get-tuple-element.31.corners_ref, f32[5]{0:T(128)} %trial_ref.5, s32[1]{0:T(128)S(6)} %copy.17.accept_ref, ...), custom_call_target="tpu_custom_call" | custom-call | tf_op jit(solution)/shard_map/spread/pallas_call | solution.py:958
  91.2 41.1 %bend.1 = (f32[128,128]{1,0:T(8,128)}, f32[2,128]{1,0:T(2,128)}) custom-call(s32[8,128]{1,0:T(8,128)} %get-tuple-element.36.corner_smem, f32[5]{0:T(128)} %trial_ref.5, bf16[64,16,128]{2,1,0:T(8,128)(2,1)} %get-tuple-element.37.own_ref, bf16[24,128]{1,0:T(8,128)(2,1)} %get-tuple-element.38.split_ref, bf16[256,256]{1,0:T(8,128)(2,1)} %get-tuple-element.28.kh_ref, ...), custom_call_target="tpu_custom_call" | custom-call | tf_op jit(solution)/shard_map/bend/pallas_call | solution.py:987
  132.4 1.2 slice_bitcast_fusion
  133.6 1.5 %copy.18 = f32[128,128]{1,0:T(8,128)} copy(f32[128,128]{1,0:T(8,128)} %get-tuple-element.52) | data formatting | bytes 131072

commit v4 on v3

--- a/solution.py
+++ b/solution.py
@@ -147,11 +147,28 @@
         first = here.half * count if self.halved else 0
         self.buf[here.me] = self.own[pl.ds(first, count)]
 
-    def start_piece(self, piece):
+    def start_lines(self):
+        def one(piece, carry):
+            self.place.others(lambda depth: self.line_copy(piece, depth).start())
+            return carry
+
+        lax.fori_loop(0, self.pieces, one, 0)
+
+    def start_near(self, piece):
         here = self.place
-        here.others(lambda depth: self.line_copy(piece, depth).start())
         self.side_copy(piece, here.depth, mine=True).start()
         self.twin_copy(piece, here.depth, here.side, mine=True).start()
+
+    def start_all_near(self):
+        def one(piece, carry):
+            self.start_near(piece)
+            return carry
+
+        lax.fori_loop(0, self.pieces, one, 0)
+
+    def start_piece(self, piece):
+        self.place.others(lambda depth: self.line_copy(piece, depth).start())
+        self.start_near(piece)
 
     def start_own(self):
         def one(piece, carry):
@@ -359,38 +376,15 @@
     planes_ref[...] = rows[...].astype(BF16).reshape(planes_ref.shape)
 
 
-def planes_kernel(
-    weights_ref,
-    direction_ref,
-    kern_x_ref,
-    kern_y_ref,
-    kern_z_ref,
-    corner_ref,
-    offsets_ref,
-    out_u,
-    out_d,
-    kh_ref,
-    kl_ref,
-    packed_ref,
-    offs_ref,
-    rows,
-    rows_d,
-):
-    slab = weights_ref.shape[0]
-    kern_y, kern_z = two_parts(kern_y_ref[...]), two_parts(kern_z_ref[...])
-    mix_planes(lambda x: weights_ref[x], kern_y, kern_z, rows, out_u, slab)
-    mix_planes(lambda x: direction_ref[x], kern_y, kern_z, rows_d, out_d, slab)
-    packed = corner_ref[0:1] + corner_ref[1:2] * 256 + corner_ref[2:3] * 65536
-    packed_ref[...] = jnp.broadcast_to(packed, packed_ref.shape)
-    offs_ref[...] = offsets_ref[...].astype(jnp.int16)
-    size_x, wide = kern_x_ref.shape[0], kh_ref.shape[1]
+def widen_kern(kern_x, slab, kh_ref, kl_ref):
+    size_x, wide = kern_x.shape[0], kh_ref.shape[1]
     group = kh_ref.shape[0] // size_x
     pack = group * slab
     source = lax.broadcasted_iota(jnp.int32, (size_x, wide), 0)
     column = lax.broadcasted_iota(jnp.int32, (size_x, wide), 1)
     same = source == lax.div(column, pack) * slab + lax.rem(column, slab)
     layer = lax.div(lax.rem(column, pack), slab)
-    for part, out_ref in zip(two_parts(kern_x_ref[...]), (kh_ref, kl_ref)):
+    for part, out_ref in zip(two_parts(kern_x), (kh_ref, kl_ref)):
         for g in range(group):
             select = jnp.where(same & (layer == g), 1.0, 0.0).astype(BF16)
             spot = jnp.dot(part, select, preferred_element_type=F32)
@@ -467,13 +461,11 @@
     group,
     trial_ref,
     accept_ref,
-    own_u,
-    own_d,
-    packed_ref,
-    offs_ref,
-    kh_ref,
-    kl_ref,
+    corner_ref,
     offsets_ref,
+    kern_x_ref,
+    kern_y_ref,
+    kern_z_ref,
     labels_ref,
     weights_ref,
     direction_ref,
@@ -486,6 +478,12 @@
     pair_offsets,
     all_offs,
     all_terms,
+    kh_ref,
+    kl_ref,
+    own_u,
+    own_d,
+    packed_ref,
+    offs_ref,
     buf_u,
     buf_d,
     all_packed,
@@ -522,6 +520,7 @@
     slab, size_y, size_z = weights_ref.shape
     half_z, size_x, _ = image_u.shape
     place = Place(devices)
+    place.greet()
     load = pltpu.make_async_copy(interp_ref, interp, local_sem.at[0])
     load.start()
     u = Relay(place, own_u, buf_u, sems[0:4], halved=True)
@@ -540,24 +539,32 @@
         swap(rows_u, mate_u, 3),
         swap(rows_d, mate_d, 4),
     ]
-    place.greet()
-    for relay in (c, u, d, o):
-        relay.keep_own()
+    kern_y, kern_z = two_parts(kern_y_ref[...]), two_parts(kern_z_ref[...])
+    packed = corner_ref[0:1] + corner_ref[1:2] * 256 + corner_ref[2:3] * 65536
+    packed_ref[...] = jnp.broadcast_to(packed, packed_ref.shape)
+    offs_ref[...] = offsets_ref[...].astype(jnp.int16)
+    mix_planes(lambda x: weights_ref[x], kern_y, kern_z, weights_t, own_u, slab)
     pair_offsets[pl.ds(0, blocks)] = offsets_ref[...]
-    for x in range(slab):
-        weights_t[pl.ds(x, size_z, stride=slab), :] = jnp.transpose(weights_ref[x])
-        direction_t[pl.ds(x, size_z, stride=slab), :] = jnp.transpose(direction_ref[x])
+    widen_kern(kern_x_ref[...], slab, kh_ref, kl_ref)
     place.meet()
     c.start_own()
     u.start_own()
     swaps[0].start()
+    mix_planes(lambda x: direction_ref[x], kern_y, kern_z, direction_t, own_d, slab)
+    for relay in (c, u, d, o):
+        relay.keep_own()
+    for x in range(slab):
+        weights_t[pl.ds(x, size_z, stride=slab), :] = jnp.transpose(weights_ref[x])
+        direction_t[pl.ds(x, size_z, stride=slab), :] = jnp.transpose(direction_ref[x])
+    d.start_lines()
+    o.start_lines()
 
     def mixer(relay, image):
         return lambda piece: mix_depth(
             relay.buf, kh_ref, kl_ref, image, group, size_x, piece * relay.size, relay.size
         )
 
-    u.run(mix=mixer(u, image_u), tail=d.start_own, riders=(c,))
+    u.run(mix=mixer(u, image_u), tail=d.start_all_near, riders=(c,))
     swaps[0].wait()
     pair_offsets[pl.ds(blocks, blocks)] = mate_offs[...].astype(jnp.int32)
     corners = all_packed[:, 0, :]
@@ -590,14 +597,14 @@
             out_u[...] = theirs[...].astype(BF16)
             rows_u[...] = image_u[:, mate_rows, :].reshape(both).astype(BF16)
 
-    d.run(work=early, steps=steps, mix=mixer(d, image_d))
+    d.run(work=early, steps=steps, mix=mixer(d, image_d), tail=o.start_all_near)
     swaps[1].start()
     pick(image_d, theirs, 0, blocks)
     out_d[...] = theirs[...].astype(BF16)
     rows_d[...] = image_d[:, mate_rows, :].reshape(both).astype(BF16)
     pick(image_d, mine_d, 0, blocks // 4)
     swaps[2].start()
-    o.start_own()
+    o.line_events(0)
     pick(image_d, mine_d, blocks // 4, blocks - blocks // 4)
     swaps[1].wait()
     mine_u[...] = mine_u[...] + in_u[...].astype(F32)
@@ -626,13 +633,12 @@
         apply_interp((mine_u, mine_d), interp, (latent_ref, slope_ref), piece * part, part)
         if piece > 0:
             t.start_piece(0)
-            o.line_events(0)
+            o.side_events(0)
         prob = jax.nn.sigmoid(latent_ref[rows] + trial_ref[accept_ref[0]] * slope_ref[rows])
         prob_ref[rows] = prob
         res_ref[rows] = (target[rows] - prob).astype(BF16).astype(F32)
         back(piece * part)
         own_terms[rows] = theirs[rows].astype(BF16)
-    o.side_events(0)
     t.keep_own()
     for relay in (c, u, d):
         relay.finish()
@@ -863,31 +869,26 @@
     point_shape = jax.ShapeDtypeStruct((blocks, per_block), F32)
 
     wide_shape = jax.ShapeDtypeStruct((group * size_x, devices * pack), BF16)
-    planes_w, planes_d, kern_high, kern_low, packed, offs = pl.pallas_call(
-        planes_kernel,
-        in_specs=[vmem] * 7,
-        out_specs=[vmem] * 6,
-        out_shape=[
-            planes_shape,
-            planes_shape,
-            wide_shape,
-            wide_shape,
-            jax.ShapeDtypeStruct((8, blocks), jnp.int32),
-            jax.ShapeDtypeStruct((blocks, cols), jnp.int16),
-        ],
-        scratch_shapes=[rows_scratch, rows_scratch],
-        compiler_params=pltpu.CompilerParams(**limit),
-        name="planes",
-    )(grid_weights, direction, kern_x, kern_y, kern_z, block_corner, block_offsets)
-
+    chunk_scratch = pltpu.VMEM((units, pack, size_y), BF16)
     pick_scratch = pltpu.VMEM((blocks, cols), F32)
     swap_scratch = pltpu.VMEM((blocks, cols), BF16)
     mate_scratch = pltpu.VMEM((size_z // 2 * slab, size_y), BF16)
-    probability, split, block_list, corners, pair_packed, pair_offsets, offsets, terms = (
+    (
+        probability,
+        split,
+        block_list,
+        corners,
+        pair_packed,
+        pair_offsets,
+        offsets,
+        terms,
+        kern_high,
+        kern_low,
+    ) = (
         pl.pallas_call(
             functools.partial(forward_kernel, group),
-            in_specs=[smem] * 2 + [vmem] * 10 + [hbm],
-            out_specs=[vmem] * 8,
+            in_specs=[smem] * 2 + [vmem] * 8 + [hbm],
+            out_specs=[vmem] * 10,
             out_shape=[
                 point_shape,
                 jax.ShapeDtypeStruct((24, 128), BF16),
@@ -897,8 +898,14 @@
                 jax.ShapeDtypeStruct((2 * blocks, cols), jnp.int32),
                 jax.ShapeDtypeStruct((devices, blocks, cols), jnp.int16),
                 jax.ShapeDtypeStruct((devices, blocks, cols), BF16),
+                wide_shape,
+                wide_shape,
             ],
             scratch_shapes=[
+                chunk_scratch,
+                chunk_scratch,
+                pltpu.VMEM((8, blocks), jnp.int32),
+                pltpu.VMEM((blocks, cols), jnp.int16),
                 planes_scratch,
                 planes_scratch,
                 pltpu.VMEM((devices, 8, blocks), jnp.int32),
@@ -941,13 +948,11 @@
         )(
             trial_steps,
             accept,
-            planes_w,
-            planes_d,
-            packed,
-            offs,
-            kern_high,
-            kern_low,
+            block_corner,
             block_offsets,
+            kern_x,
+            kern_y,
+            kern_z,
             labels,
             grid_weights,
             direction,

time: 135 us -> 131 us (0.970); the launches traced: 135 us -> 130 us
  Pallas kernels: 131 us -> 126 us
    pallas_call x1 -> x0, Pallas kernels: 4.12 us -> none  [body(): pl.pallas_call(planes_kernel, in_specs=[vmem] * 7, out_specs=[vmem] * 6,...]
    pallas_call x1, Pallas kernels: 78.3 us -> 76.5 us  [body(): pl.pallas_call(functools.partial(forward_kernel, group), in_specs=[smem]...]
where the time goes in v4:
time: 131 us; the launch traced here: 130 us
  Pallas kernels  126 us (96%)
  local copies, waits for them, and re-layouts  2.73 us (2%)
    pallas_call x1, Pallas kernels, body(): pl.pallas_call(functools.partial(forward_kernel, group), in_specs=[smem]...  76.5 us
    pallas_call x1, Pallas kernels, body(): pl.pallas_call(functools.partial(bend_kernel, group, points), in_specs=[s...  41 us
    pallas_call x1, Pallas kernels, body(): pl.pallas_call(spread_kernel, in_specs=[smem] * 4 + [vmem] * 6, out_specs...  8.12 us

profile of v4, /device:TPU:0, one launch (start us, length us, event | category | flops | bytes accessed | tf_op | source)
XLA Modules:
  0.0 129.6 jit_solution(11641438637327406375)
XLA Ops:
  1.3 76.5 %forward.1 = (f32[128,128]{1,0:T(8,128)}, bf16[24,128]{1,0:T(8,128)(2,1)}, s32[24,128]{1,0:T(8,128)}, s32[16,128]{1,0:T(8,128)}, s32[8,128]{1,0:T(8,128)}, /*ind...) custom-call(f32[5]{0:T(128)} %trial_ref.5, ...), custom_call_target="tpu_custom_call" | custom-call | tf_op jit(solution)/shard_map/forward/pallas_call | solution.py:888
  77.8 8.1 %spread.1 = (f32[8,128,128]{2,1,0:T(8,128)}, f32[8,128,128]{2,1,0:T(8,128)}, bf16[64,16,128]{2,1,0:T(8,128)(2,1)}) custom-call(s32[24,128]{1,0:T(8,128)} %get-tuple-element.20.list_ref, s32[16,128]{1,0:T(8,128)} %get-tuple-element.21.corners_ref, f32[5]{0:T(128)} %trial_ref.5, s32[1]{0:T(128)S(6)} %copy.17.accept_ref, ...), custom_call_target="tpu_custom_call" | custom-call | tf_op jit(solution)/shard_map/spread/pallas_call | solution.py:963
  85.9 41.0 %bend.1 = (f32[128,128]{1,0:T(8,128)}, f32[2,128]{1,0:T(2,128)}) custom-call(s32[8,128]{1,0:T(8,128)} %get-tuple-element.26.corner_smem, f32[5]{0:T(128)} %trial_ref.5, bf16[64,16,128]{2,1,0:T(8,128)(2,1)} %get-tuple-element.27.own_ref, bf16[24,128]{1,0:T(8,128)(2,1)} %get-tuple-element.28.split_ref, bf16[256,256]{1,0:T(8,128)(2,1)} %get-tuple-element.29.kh_ref, ...), custom_call_target="tpu_custom_call" | custom-call | tf_op jit(solution)/shard_map/bend/pallas_call | solution.py:992
  126.9 1.3 slice_bitcast_fusion
  128.1 1.5 %copy.18 = f32[128,128]{1,0:T(8,128)} copy(f32[128,128]{1,0:T(8,128)} %get-tuple-element.44) | data formatting | bytes 131072

commit v5 on v4

--- a/solution.py
+++ b/solution.py
@@ -206,7 +206,16 @@
 
         lax.fori_loop(0, here.devices // 2, one, 0)
 
-    def run(self, work=None, steps=0, mix=None, tail=None, riders=()):
+    def head(self, wave):
+        @pl.when(wave < self.pieces)
+        def _():
+            self.line_events(wave)
+
+        @pl.when(wave == 1)
+        def _():
+            self.side_events(0)
+
+    def run(self, first=0, work=None, steps=0, mix=None, tail=None, riders=(), follow=None):
         pieces = self.pieces
 
         def one(wave, carry):
@@ -230,7 +239,7 @@
 
             if tail is not None:
 
-                @pl.when(wave == pieces - 1)
+                @pl.when(wave == max(first, pieces - 1))
                 def _():
                     tail()
 
@@ -238,11 +247,17 @@
             def _():
                 self.side_events(wave - 1)
 
+            if follow is not None:
+
+                @pl.when(wave >= pieces)
+                def _():
+                    follow.head(wave - pieces)
+
             if work is not None:
 
-                @pl.when(wave < steps)
+                @pl.when(wave - first < steps)
                 def _():
-                    work(wave)
+                    work(wave - first)
 
             @pl.when(wave >= 2)
             def _():
@@ -252,7 +267,7 @@
 
             return carry
 
-        lax.fori_loop(0, pieces + 2, one, 0)
+        lax.fori_loop(first, pieces + 2, one, 0)
 
     def finish(self):
         here = self.place
@@ -564,18 +579,46 @@
             relay.buf, kh_ref, kl_ref, image, group, size_x, piece * relay.size, relay.size
         )
 
-    u.run(mix=mixer(u, image_u), tail=d.start_all_near, riders=(c,))
+    last = u.pieces + 1
+    to_smem = pltpu.make_async_copy(pair_packed, corner_smem, local_sem.at[1])
+
+    def list_lines(first, count):
+        def one(line, carry):
+            list_blocks(ranks_ref, list_ref, line)
+            return carry
+
+        lax.fori_loop(first, first + count, one, 0)
+
+    def prepare(wave):
+        @pl.when(wave == 2)
+        def _():
+            corners = all_packed[:, 0, :]
+            corners_ref[...] = corners
+            pair_packed[...] = jnp.concatenate(
+                [packed_ref[0:4], all_packed[place.mate, 0:4]], axis=0
+            )
+            rank_blocks(corners, place.me, slab, ranks_ref, list_ref)
+            to_smem.start()
+
+        for k in range(2):
+
+            @pl.when(wave == min(3 + k, last))
+            def _():
+                list_lines(devices // 2 * k, devices // 2)
+
+    u.run(
+        work=prepare,
+        steps=last + 1,
+        mix=mixer(u, image_u),
+        tail=d.start_all_near,
+        riders=(c,),
+        follow=d,
+    )
     swaps[0].wait()
     pair_offsets[pl.ds(blocks, blocks)] = mate_offs[...].astype(jnp.int32)
-    corners = all_packed[:, 0, :]
-    corners_ref[...] = corners
-    pair_packed[...] = jnp.concatenate([packed_ref[0:4], all_packed[place.mate, 0:4]], axis=0)
-    rank_blocks(corners, place.me, slab, ranks_ref, list_ref)
-    to_smem = pltpu.make_async_copy(pair_packed, corner_smem, local_sem.at[1])
-    to_smem.start()
     to_smem.wait()
-    steps = power_below(u.pieces + 2)
-    some, lines = blocks // steps, -(-devices // steps)
+    steps = power_below(u.pieces)
+    some = blocks // steps
 
     def pick(image, mine, first, count):
         line, base = (0, 0) if mine is not theirs else (4, blocks)
@@ -589,29 +632,26 @@
     def early(step):
         pick(image_u, theirs, step * some, some)
         pick(image_u, mine_u, step * some, some)
-        for k in range(lines):
-            list_blocks(ranks_ref, list_ref, step * lines + k)
 
         @pl.when(step == steps - 1)
         def _():
             out_u[...] = theirs[...].astype(BF16)
             rows_u[...] = image_u[:, mate_rows, :].reshape(both).astype(BF16)
 
-    d.run(work=early, steps=steps, mix=mixer(d, image_d), tail=o.start_all_near)
+    d.run(first=2, work=early, steps=steps, mix=mixer(d, image_d), tail=o.start_all_near)
     swaps[1].start()
     pick(image_d, theirs, 0, blocks)
     out_d[...] = theirs[...].astype(BF16)
     rows_d[...] = image_d[:, mate_rows, :].reshape(both).astype(BF16)
     pick(image_d, mine_d, 0, blocks // 4)
-    swaps[2].start()
+    for k in (2, 3, 4):
+        swaps[k].start()
     o.line_events(0)
     pick(image_d, mine_d, blocks // 4, blocks - blocks // 4)
     swaps[1].wait()
     mine_u[...] = mine_u[...] + in_u[...].astype(F32)
     load.wait()
     swaps[2].wait()
-    swaps[3].start()
-    swaps[4].start()
     mine_d[...] = mine_d[...] + in_d[...].astype(F32)
     target = labels_ref[...].astype(F32)
     part = blocks // 2

time: 131 us -> 127 us (0.969); the launches traced: 130 us -> 127 us
  Pallas kernels: 126 us -> 123 us
    pallas_call x1, Pallas kernels: 76.5 us -> 73.5 us  [body(): pl.pallas_call(functools.partial(forward_kernel, group), in_specs=[smem]...]
    pallas_call x1, Pallas kernels: 41 us -> 42.4 us  [body(): pl.pallas_call(functools.partial(bend_kernel, group, points), in_specs=[s...]
where the time goes in v5:
time: 127 us
  Pallas kernels  123 us (97%)
  local copies, waits for them, and re-layouts  2.73 us (2%)
  between operations  1.3 us (1%)
    pallas_call x1, Pallas kernels, body(): pl.pallas_call(functools.partial(forward_kernel, group), in_specs=[smem]...  73.5 us
    pallas_call x1, Pallas kernels, body(): pl.pallas_call(functools.partial(bend_kernel, group, points), in_specs=[s...  42.4 us
    pallas_call x1, Pallas kernels, body(): pl.pallas_call(spread_kernel, in_specs=[smem] * 4 + [vmem] * 6, out_specs...  7.49 us

profile of v5, /device:TPU:0, one launch (start us, length us, event | category | flops | bytes accessed | tf_op | source)
XLA Modules:
  0.0 127.4 jit_solution(6148146436265092974)
XLA Ops:
  1.3 73.5 %forward.1 = (f32[128,128]{1,0:T(8,128)}, bf16[24,128]{1,0:T(8,128)(2,1)}, s32[24,128]{1,0:T(8,128)}, s32[16,128]{1,0:T(8,128)}, s32[8,128]{1,0:T(8,128)}, /*ind...) custom-call(f32[5]{0:T(128)} %trial_ref.5, ...), custom_call_target="tpu_custom_call" | custom-call | tf_op jit(solution)/shard_map/forward/pallas_call | solution.py:928
  74.8 7.5 %spread.1 = (f32[8,128,128]{2,1,0:T(8,128)}, f32[8,128,128]{2,1,0:T(8,128)}, bf16[64,16,128]{2,1,0:T(8,128)(2,1)}) custom-call(s32[24,128]{1,0:T(8,128)} %get-tuple-element.20.list_ref, s32[16,128]{1,0:T(8,128)} %get-tuple-element.21.corners_ref, f32[5]{0:T(128)} %trial_ref.5, s32[1]{0:T(128)S(6)} %copy.17.accept_ref, ...), custom_call_target="tpu_custom_call" | custom-call | tf_op jit(solution)/shard_map/spread/pallas_call | solution.py:1003
  82.3 42.4 %bend.1 = (f32[128,128]{1,0:T(8,128)}, f32[2,128]{1,0:T(2,128)}) custom-call(s32[8,128]{1,0:T(8,128)} %get-tuple-element.26.corner_smem, f32[5]{0:T(128)} %trial_ref.5, bf16[64,16,128]{2,1,0:T(8,128)(2,1)} %get-tuple-element.27.own_ref, bf16[24,128]{1,0:T(8,128)(2,1)} %get-tuple-element.28.split_ref, bf16[256,256]{1,0:T(8,128)(2,1)} %get-tuple-element.29.kh_ref, ...), custom_call_target="tpu_custom_call" | custom-call | tf_op jit(solution)/shard_map/bend/pallas_call | solution.py:1032
  124.7 1.3 slice_bitcast_fusion
  125.9 1.5 %copy.18 = f32[128,128]{1,0:T(8,128)} copy(f32[128,128]{1,0:T(8,128)} %get-tuple-element.44) | data formatting | bytes 131072

commit v6 on v5

--- a/solution.py
+++ b/solution.py
@@ -1046,7 +1046,7 @@
             pltpu.SemaphoreType.DMA,
             pltpu.SemaphoreType.DMA,
             pltpu.SemaphoreType.DMA,
-            *relay_sems(devices, pieces),
+            *relay_sems(devices, max(1, pieces // 2)),
             *relay_sems(devices, 1),
         ],
         compiler_params=pltpu.CompilerParams(collective_id=1, has_side_effects=True, **limit),

time: 127 us -> 127 us (level)
  no operation moved by 1% of the time
where the time goes in v6:
time: 127 us
  Pallas kernels  123 us (97%)
  local copies, waits for them, and re-layouts  2.73 us (2%)
  between operations  1.3 us (1%)
    pallas_call x1, Pallas kernels, body(): pl.pallas_call(functools.partial(forward_kernel, group), in_specs=[smem]...  73.6 us
    pallas_call x1, Pallas kernels, body(): pl.pallas_call(functools.partial(bend_kernel, group, points), in_specs=[s...  42.1 us
    pallas_call x1, Pallas kernels, body(): pl.pallas_call(spread_kernel, in_specs=[smem] * 4 + [vmem] * 6, out_specs...  7.51 us

profile of v6, /device:TPU:0, one launch (start us, length us, event | category | flops | bytes accessed | tf_op | source)
XLA Modules:
  0.0 127.2 jit_solution(7793351625659301879)
XLA Ops:
  1.3 73.6 %forward.1 = (f32[128,128]{1,0:T(8,128)}, bf16[24,128]{1,0:T(8,128)(2,1)}, s32[24,128]{1,0:T(8,128)}, s32[16,128]{1,0:T(8,128)}, s32[8,128]{1,0:T(8,128)}, /*ind...) custom-call(f32[5]{0:T(128)} %trial_ref.5, ...), custom_call_target="tpu_custom_call" | custom-call | tf_op jit(solution)/shard_map/forward/pallas_call | solution.py:928
  74.8 7.5 %spread.1 = (f32[8,128,128]{2,1,0:T(8,128)}, f32[8,128,128]{2,1,0:T(8,128)}, bf16[64,16,128]{2,1,0:T(8,128)(2,1)}) custom-call(s32[24,128]{1,0:T(8,128)} %get-tuple-element.20.list_ref, s32[16,128]{1,0:T(8,128)} %get-tuple-element.21.corners_ref, f32[5]{0:T(128)} %trial_ref.5, s32[1]{0:T(128)S(6)} %copy.17.accept_ref, ...), custom_call_target="tpu_custom_call" | custom-call | tf_op jit(solution)/shard_map/spread/pallas_call | solution.py:1003
  82.3 42.1 %bend.1 = (f32[128,128]{1,0:T(8,128)}, f32[2,128]{1,0:T(2,128)}) custom-call(s32[8,128]{1,0:T(8,128)} %get-tuple-element.26.corner_smem, f32[5]{0:T(128)} %trial_ref.5, bf16[64,16,128]{2,1,0:T(8,128)(2,1)} %get-tuple-element.27.own_ref, bf16[24,128]{1,0:T(8,128)(2,1)} %get-tuple-element.28.split_ref, bf16[256,256]{1,0:T(8,128)(2,1)} %get-tuple-element.29.kh_ref, ...), custom_call_target="tpu_custom_call" | custom-call | tf_op jit(solution)/shard_map/bend/pallas_call | solution.py:1032
  124.5 1.3 slice_bitcast_fusion
  125.7 1.5 %copy.18 = f32[128,128]{1,0:T(8,128)} copy(f32[128,128]{1,0:T(8,128)} %get-tuple-element.44) | data formatting | bytes 131072
